TPU v7x, 128 devices: a whole 4x4x4 slice. The times are simulated.
128 devices in a mesh: seq: 4 (over x_lo, core), tensor: 32 (over z, y, x_hi).
Axes of the slice: x: 4 (x_hi: 2, x_lo: 2; x = x_hi * 2 + x_lo), y: 4, z: 4, core: 2. Of those that a mesh axis runs over, the one named last changes fastest.
Arguments:
- tokens: bfloat16 [2, 4096, 4096], P(None, 'seq', 'tensor'), may hold values from -6 to 6
- w_qkv: bfloat16 [4096, 3, 4096], P(None, None, 'tensor'), may hold values from -1 to 1
- q_gain: float32 [4096], P('tensor'), may hold values from 0.5 to 2.5
- k_gain: float32 [4096], P('tensor'), may hold values from 0.5 to 2.5
- w_out: bfloat16 [4096, 4096], P('tensor'), may hold values from -0.1875 to 0.1875
Outputs:
- mixed: bfloat16 [2, 4096, 4096], P(None, 'seq', 'tensor')
- peak: float32 [32], P('tensor')
- qk_scale: float32 [2, 2, 4096], P(None, None, 'seq')
All inputs are finite; a program needn't handle non-finite values.
Results may differ from a plain program's by a relative error of at most 0.024.
Values may be sent and summed in bfloat16 or wider, within the bound.
No kernel may reach another device: no remote copies, remote signals or barrier semaphores. Data moves between devices by JAX's collectives and lax.ppermute only.
A program may use at most 128 MiB of HBM per device.

v0:
```python
import jax
import jax.numpy as jnp
from jax import lax
from jax.sharding import Mesh
from jax.sharding import PartitionSpec as P

HEADS = 32
TENSOR = ("tensor_0", "tensor_1", "tensor_2")


EPS = 1e-06
ROPE_BASE = 500000.0
NEG = -1e30


def sent_to_all(array, axis):
    size = lax.axis_size(axis)
    return lax.all_to_all(
        jnp.broadcast_to(array[None], (size, *array.shape)), axis, 0, 0, tiled=True
    )


def taken_together(array, axis):
    return sent_to_all(array, axis).sum(axis=0)


def side_by_side(arrays, axis, dim, along):
    both = jnp.concatenate(arrays, axis=along)
    filled, at, gathered = (lax.all_gather(both, axis, axis=dim, tiled=True), 0, [])
    for a in arrays:
        gathered.append(lax.slice_in_dim(filled, at, at + a.shape[along], axis=along))
        at += a.shape[along]
    return tuple(gathered)


def over_copies(array, axis):
    return sent_to_all(array, axis).max(axis=0)


def sum_by_axis(array, axes, dim):
    for axis in axes:
        array = lax.psum_scatter(array, axis, scatter_dimension=dim, tiled=True)
    return array


def rope_tables(positions, head):
    half = head // 2
    freq = ROPE_BASE ** (-(jnp.arange(half, dtype=jnp.float32) * 2.0) / head)
    angle = positions[:, None] * freq[None, :]
    return (jnp.cos(angle), jnp.sin(angle))


def rotate(values, cosine, sine):
    half = values.shape[-1] // 2
    first = values[..., :half]
    second = values[..., half:]
    cosine = cosine[:, None, :]
    sine = sine[:, None, :]
    return jnp.concatenate([first * cosine - second * sine, second * cosine + first * sine], -1)


def norm_stats(query, keyed, width):
    totals = taken_together(
        jnp.stack([jnp.sum(query * query, 1), jnp.sum(keyed * keyed, 1)]), TENSOR
    )
    return lax.rsqrt(totals / width + EPS)


def online_update(q_part, k_part, v_part, valid, state, scale):
    top, denom, accum = state
    scores = jnp.einsum("sqd,skd->sqk", q_part, k_part, preferred_element_type=jnp.float32) * scale
    scores = jnp.where(valid[None], scores, NEG)
    new_top = jnp.maximum(top, jnp.max(scores, -1))
    weights = jnp.where(valid[None], jnp.exp(scores - new_top[..., None]), 0.0)
    factor = jnp.exp(top - new_top)
    added = jnp.einsum(
        "sqk,skd->sqd", weights.astype(jnp.bfloat16), v_part, preferred_element_type=jnp.float32
    )
    return (new_top, denom * factor + jnp.sum(weights, -1), accum * factor[..., None] + added)


def shards(tokens, w_qkv, q_gain, k_gain, w_out):
    seqs, tok, dloc = tokens.shape
    width = w_qkv.shape[0]
    head = width // HEADS
    heads_here = dloc // head
    rows = seqs * tok
    flat_w = w_qkv.reshape(width, 3 * dloc)
    whole = lax.all_gather(tokens, TENSOR, axis=2, tiled=True).reshape(rows, width)
    paired = jnp.dot(whole, flat_w[:, : 2 * dloc], preferred_element_type=jnp.float32)
    query = paired[:, :dloc]
    keyed = paired[:, dloc:]
    inverse = norm_stats(query, keyed, width)
    value = jnp.dot(whole, flat_w[:, 2 * dloc :], preferred_element_type=jnp.float32)
    own_index = lax.axis_index("seq")
    q_index = own_index * tok + jnp.arange(tok, dtype=jnp.int32)
    cosine, sine = rope_tables(q_index.astype(jnp.float32), head)

    def prepare(projection, scale_row, gain):
        normed = projection * scale_row[:, None] * gain[None, :]
        return rotate(normed.reshape(seqs, tok, heads_here, head), cosine, sine).astype(
            jnp.bfloat16
        )

    q_heads = prepare(query, inverse[0], q_gain).transpose(2, 0, 1, 3)
    k_ready = prepare(keyed, inverse[1], k_gain).reshape(seqs, tok, dloc)
    v_ready = value.astype(jnp.bfloat16).reshape(seqs, tok, dloc)
    scale = head ** (-0.5)
    keys_all, values_all = side_by_side((k_ready, v_ready), "seq", 1, 0)
    total_len = keys_all.shape[1]
    k_heads = keys_all.reshape(seqs, total_len, heads_here, head).transpose(2, 0, 1, 3)
    v_heads = values_all.reshape(seqs, total_len, heads_here, head).transpose(2, 0, 1, 3)

    def attend(operands):
        q_one, k_one, v_one = operands

        def visit(step, state):
            first = step * tok
            k_part = lax.dynamic_slice_in_dim(k_one, first, tok, 1)
            v_part = lax.dynamic_slice_in_dim(v_one, first, tok, 1)
            valid = (first + jnp.arange(tok, dtype=jnp.int32))[None, :] <= q_index[:, None]
            return online_update(q_one, k_part, v_part, valid, state, scale)

        initial = (
            jnp.full((seqs, tok), NEG, jnp.float32),
            jnp.zeros((seqs, tok), jnp.float32),
            jnp.zeros((seqs, tok, head), jnp.float32),
        )
        top, denom, accum = lax.fori_loop(0, own_index + 1, visit, initial)
        return (accum / denom[..., None], top)

    outputs, tops = lax.map(attend, (q_heads, k_heads, v_heads))
    attended = outputs.astype(jnp.bfloat16).transpose(1, 2, 0, 3).reshape(rows, dloc)
    peak = over_copies(jnp.max(tops, axis=(1, 2)), "seq")
    partial_out = (
        jnp.dot(attended, w_out, preferred_element_type=jnp.float32)
        .astype(jnp.bfloat16)
        .reshape(seqs, tok, width)
    )
    mixed = sum_by_axis(partial_out, TENSOR, 2).astype(jnp.float32)
    return (mixed.astype(jnp.bfloat16), peak, inverse.reshape(2, seqs, tok))


def solution(mesh):
    finer = Mesh(
        mesh.devices.reshape(mesh.shape["seq"], 4, 4, 2),
        ("seq", "tensor_0", "tensor_1", "tensor_2"),
    )
    placed = (P(None, "seq", TENSOR), P(None, None, TENSOR), P(TENSOR), P(TENSOR), P(TENSOR, None))
    return jax.shard_map(
        shards,
        mesh=finer,
        in_specs=placed,
        out_specs=(P(None, "seq", TENSOR), P(TENSOR), P(None, None, "seq")),
        check_vma=False,
    )
```

profile of v0, /device:TPU:1, one launch (start us, length us, event | category | flops | bytes accessed | tf_op | source)
XLA Modules:
  0.0 593.4 jit_solution(10021887254225840839)
XLA Ops:
  7.9 4.7 copy.16
  12.7 3.1 multiply_cosine_fusion
  15.7 205.0 %all-gather.3.cloned.1.call-done = bf16[2,1024,4096]{2,1,0:T(8,128)(2,1)} async-done(((bf16[2,1024,128]{2,1,0:T(8,128)(2,1)}), bf16[2,1024,4096]{2,1,0:T(8,128)(2,1)}) %all-gather.3.cloned.1.call-update) | async-done | bytes 16777232 | tf_op jit(solution)/shard_map/all_gather | solution.py:89
  220.7 8.8 %fusion.19 = f32[2048,256]{1,0:T(8,128)S(1)} fusion(bf16[2048,4096]{1,0:T(8,128)(2,1)} %bitcast.64, bf16[4096,384]{0,1:T(8,128)(2,1)} %bitcast.55), kind=kOutput, calls=%fused_computation.24 | convolution fusion | flops 4294967296 | bytes 20971520 | tf_op jit(solution)/shard_map/dot_general | solution.py:90
  231.2 5.4 all-to-all-start
  236.7 11.3 %convolution_convert_fusion.1 = bf16[2048,128]{1,0:T(8,128)(2,1)} fusion(bf16[2048,4096]{1,0:T(8,128)(2,1)} %bitcast.65, bf16[4096,384]{0,1:T(8,128)(2,1)} %bitcast.56), kind=kOutput, calls=%fused_computation.23 | convolution fusion | flops 2147745792 | bytes 18350080 | tf_op jit(solution)/shard_map/dot_general | solution.py:94
  250.6 2.0 fusion.24
  252.5 1.3 pad_maximum_fusion
  255.1 48.1 %all-gather.5.cloned.1.call-done = bf16[4,4096,128]{2,1,0:T(8,128)(2,1)} async-done(((bf16[4,1024,128]{2,1,0:T(8,128)(2,1)}), bf16[4,4096,128]{2,1,0:T(8,128)(2,1)}) %all-gather.5.cloned.1.call-update) | async-done | bytes 4194320 | tf_op jit(solution)/shard_map/all_gather | solution.py:29
  303.3 4.5 fusion.26
  307.8 21.6 %while.25 = (s32[]{:T(128)}, f32[2,1024]{1,0:T(2,128)S(1)}, f32[2,1024]{1,0:T(2,128)S(1)}, f32[2,1024,128]{2,1,0:T(8,128)S(1)}, s32[]{:T(128)}, /*index=5*/bf16[...) while((s32[]{:T(128)}, f32[2,1024]{1,0:T(2,128)S(1)}, ...), condition=%wide.region_6.7_spmd.clone, body=%wide.region_3.6_spmd.clone.sunk | while | flops 1102583808 | bytes 33177796 | solution.py:129
  308.5 3.0 fusion.42
  311.5 2.3 fusion.43
  313.8 4.8 fusion.44
  319.3 3.0 fusion.42
  322.3 2.3 fusion.43
  324.6 4.8 fusion.44
  329.7 8.0 %convolution_convert_fusion = bf16[2048,4096]{1,0:T(8,128)(2,1)} fusion(bf16[2048,128]{1,0:T(8,128)(2,1)S(1)} %bitcast.57, bf16[128,4096]{1,0:T(8,128)(2,1)S(1)} %copy-done), kind=kOutput, calls=%fused_computation.22 | convolution fusion | flops 2155872256 | bytes 18350080 | tf_op jit(solution)/shard_map/dot_general | solution.py:136
  337.9 169.6 %reduce-scatter.6.cloned.1.call-done = bf16[2,1024,1024]{2,1,0:T(8,128)(2,1)} async-done(((bf16[2,1024,4096]{2,1,0:T(8,128)(2,1)}), bf16[2,1024,1024]{2,1,0:T(8,128)(2,1)}) %reduce-scatter.6.cloned.1.call-update) | async-done | bytes 4194320 | tf_op jit(solution)/shard_map/reduce_scatter | solution.py:42
  507.6 48.6 %reduce-scatter.8.cloned.1.call-done = bf16[2,1024,256]{2,1,0:T(8,128)(2,1)} async-done(((bf16[2,1024,1024]{2,1,0:T(8,128)(2,1)}), bf16[2,1024,256]{2,1,0:T(8,128)(2,1)}) %reduce-scatter.8.cloned.1.call-update) | async-done | bytes 1048592 | tf_op jit(solution)/shard_map/reduce_scatter | solution.py:42
  556.2 2.6 copy.20
  562.0 6.4 %all_to_all.11 = f32[4,1,1]{2,1,0:T(1,128)S(1)} all-to-all(f32[4,1,1]{2,1,0:T(1,128)S(1)} %broadcast_in_dim.37), channel_id=1, replica_groups=mesh['seq'=4,'tensor_0'=4,'tensor_1'=4,'tensor_2'=2] {'seq'}, dimensions={0} | all-to-all | bytes 32 | tf_op jit(solution)/shard_map/all_to_all | solution.py:18
  568.9 15.3 %reduce-scatter.10.cloned.1.call-done = bf16[128,2048]{1,0:T(8,128)(2,1)} async-done(((bf16[256,2048]{1,0:T(8,128)(2,1)}), bf16[128,2048]{1,0:T(8,128)(2,1)}) %reduce-scatter.10.cloned.1.call-update) | async-done | bytes 524304
  584.2 1.4 reshape.187
  (49 shorter events, 13.1 us)
Async XLA Ops:
  7.2 322.6 %copy-start = (bf16[128,4096]{1,0:T(8,128)(2,1)S(1)}, bf16[128,4096]{1,0:T(8,128)(2,1)}, u32[]{:S(2)}) copy-start(bf16[128,4096]{1,0:T(8,128)(2,1)} %param.11) | copy-start | bytes 3145732
  7.2 213.6 %all-gather.3.cloned.1.call-start = ((), (), s32[]{:S(2)}) async-start(), calls=%async_computation.5 | async-start | bytes 17301504 | tf_op jit(solution)/shard_map/all_gather | solution.py:89
  231.2 17.4 %all-to-all-start = ((f32[32,2,2048]{2,1,0:T(2,128)}), f32[32,2,2048]{2,1,0:T(2,128)}, u32[]{:S(2)}, u32[]{:S(2)}) async-start(f32[32,2,2048]{2,1,0:T(2,128)} %broadcast_in_dim.36), calls=%async_computation | async-start | bytes 1048576 | tf_op jit(solution)/shard_map/all_to_all | solution.py:18
  236.6 13.2 %copy-start.2 = (f32[128]{0:T(128)S(1)}, f32[128]{0:T(128)}, u32[]{:S(2)}) copy-start(f32[128]{0:T(128)} %param.9) | copy-start | bytes 1540
  236.6 13.2 %copy-start.3 = (f32[128]{0:T(128)S(1)}, f32[128]{0:T(128)}, u32[]{:S(2)}) copy-start(f32[128]{0:T(128)} %param.10) | copy-start | bytes 1540
  236.6 66.6 %all-gather.5.cloned.1.call-start = ((), (), s32[]{:S(2)}) async-start(), calls=%async_computation.6 | async-start | bytes 5242880 | tf_op jit(solution)/shard_map/all_gather | solution.py:29
  249.8 2.8 copy-start.1
  253.8 253.7 %reduce-scatter.6.cloned.1.call-start = ((), (), s32[]{:S(2)}) async-start(), calls=%async_computation.7 | async-start | bytes 20971520 | tf_op jit(solution)/shard_map/reduce_scatter | solution.py:42
  337.8 218.4 %reduce-scatter.8.cloned.1.call-start = ((), (), s32[]{:S(2)}) async-start(), calls=%async_computation.8 | async-start | bytes 5242880 | tf_op jit(solution)/shard_map/reduce_scatter | solution.py:42
  507.5 76.7 %reduce-scatter.10.cloned.1.call-start = ((), (), s32[]{:S(2)}) async-start(), calls=%async_computation.9 | async-start | bytes 1572864
Sparse Core Ops, SparseCore 0:
  10.7 209.9 all-gather.2
  253.9 49.2 all-gather.4
  337.9 169.4 reduce-scatter.5
  509.7 46.4 reduce-scatter.7
  560.2 24.0 reduce-scatter.9
where the time goes:
time: 594 us; the launch traced here: 593 us
  waiting for transfers between devices  488 us (82%)
  matrix products  43.7 us (7%)
  local copies, waits for them, and re-layouts  18.1 us (3%)
  other arithmetic  17.4 us (3%)
  between operations  14 us (2%)
  blocking collectives  6.36 us (1%)
    reduce_scatter x2, waiting for transfers between devices, sum_by_axis(): array = lax.psum_scatter(array, axis, scatter_dimension=dim, tiled=True)  218 us
    all_gather x1, waiting for transfers between devices, shards(): lax.all_gather(tokens, TENSOR, axis=2, tiled=True).reshape(rows, width)  205 us
    all_gather x1, waiting for transfers between devices, side_by_side(): lax.all_gather(both, axis, axis=dim, tiled=True)  48.1 us
    unnamed x6, waiting for transfers between devices  16.1 us
  transfers between devices with their start and end apart: 6, of which 6 were waited for; matrix products, arithmetic and copies ran while one was open for 4% of the time, Pallas kernels for 0%

commit v1 on v0

v1 whole, which is shorter than its diff:
```python
import jax
import jax.numpy as jnp
from jax import lax
from jax.experimental import pallas as pl
from jax.experimental.pallas import tpu as pltpu
from jax.sharding import Mesh
from jax.sharding import PartitionSpec as P


TENSOR = ("z", "y", "xh")
AXES = ("xl", "c", "z", "y", "xh")
EPS = 1e-06
ROPE_BASE = 500000.0
NEG = -1e30
LOG2E = 1.4426950408889634


ROWS = 256
QB = 512
CROSS = [(0, 3), (3, 0), (1, 2), (2, 1)]


def shift(n, k):
    return [(i, (i + k) % n) for i in range(n)]


def swap(array, axis):
    return lax.ppermute(array, axis, [(0, 1), (1, 0)])


def to_all(array, axes):
    size = lax.axis_size(axes)
    return lax.all_to_all(jnp.broadcast_to(array, (size, *array.shape[1:])), axes, 0, 0, tiled=True)


def permute(array, axis, k):
    return lax.ppermute(array, axis, shift(4, k))


def ring_direct(block, axis):
    before = permute(block, axis, 1)
    after = permute(block, axis, -1)
    far = permute(block, axis, 2)
    return before, after, far


def ring_relay(own, before, after, far, axis):
    low = jnp.stack([own, before])
    high = jnp.stack([after, far])
    before_low = permute(low, axis, 1)
    after_high = permute(high, axis, -1)
    before_high = permute(high, axis, 1)
    after_low = permute(low, axis, -1)
    far_low = permute(before_low, axis, 1)
    far_high = permute(after_high, axis, -1)
    near = (low, high, before_low, before_high, after_low, after_high)
    return near, (far_low, far_high)


def rel_slot(distance):
    d = distance % 4
    return jnp.where(d == 0, 0, jnp.where(d == 1, 2, jnp.where(d == 2, 3, 1)))


def fill_weights(idx, w_loc, w_own, w_oth, w_near, w_far):
    z, y, xh, c = idx[0], idx[1], idx[2], idx[4]

    def place(t, src, at_col, w):
        iz, iy = rel_slot(t // 8 - z), rel_slot((t // 2) % 4 - y)
        same = (t % 2) == xh
        outer = jnp.where(same, iy, iz)
        inner = jnp.where(same, iz, iy)
        base = jnp.where(same, 0, 1)
        rows = pl.ds(pl.multiple_of(src * 128, 128), 128)

        @pl.when(outer < 3)
        def _():
            to = pl.ds(pl.multiple_of((base * 12 + outer * 4 + inner) * 128, 128), 128)
            for j in range(3):
                w_near[to, at_col + 128 * j : at_col + 128 * (j + 1)] = w[j, rows, :]

        @pl.when(outer == 3)
        def _():
            to = pl.ds(pl.multiple_of((base * 4 + inner) * 128, 128), 128)
            for j in range(3):
                w_far[to, at_col + 128 * j : at_col + 128 * (j + 1)] = w[j, rows, :]

    def fill(i, carry):
        place(c * 16 + i, c * 16 + i, 0, w_loc)
        place((1 - c) * 16 + i, (1 - c) * 16 + i, 0, w_loc)
        place(c * 16 + i, i, 384, w_own)
        place((1 - c) * 16 + i, i, 384, w_oth)
        return carry

    lax.fori_loop(0, 16, fill, 0)


def near_kernel(idx, *refs):
    xs, (w_loc, w_own, w_oth, out, w_far, w_near) = refs[:12], refs[12:]

    @pl.when(pl.program_id(0) == 0)
    def _():
        fill_weights(idx, w_loc, w_own, w_oth, w_near, w_far)

    blocks = [x[i] for x in xs for i in range(2)]
    out[...] = jnp.dot(jnp.concatenate(blocks, axis=1), w_near[...], preferred_element_type=jnp.float32)


def far_kernel(idx, *refs):
    xs, (acc_ref, w_far, gains, cos_ref, sin_ref) = refs[:4], refs[4:9]
    keep_a, keep_b, send, ssq = refs[9:]
    xh, xl = idx[2], idx[3]
    step = pl.program_id(0)
    blocks = [x[i] for x in xs for i in range(2)]
    acc = acc_ref[...] + jnp.dot(
        jnp.concatenate(blocks, axis=1), w_far[...], preferred_element_type=jnp.float32
    )
    q0, k0, v0 = acc[:, :128], acc[:, 128:256], acc[:, 256:384]
    q1, k1, v1 = acc[:, 384:512], acc[:, 512:640], acc[:, 640:]
    ssq[0:1, :] = jnp.sum((q0 * q0 + q1 * q1).T, axis=0, keepdims=True)
    ssq[1:2, :] = jnp.sum((k0 * k0 + k1 * k1).T, axis=0, keepdims=True)
    cosine, sine = cos_ref[...], sin_ref[...]

    def rope(value, gain):
        value = value * gain
        return (value * cosine + pltpu.roll(value, 64, 1) * sine).astype(jnp.bfloat16)

    loc = (rope(q0, gains[0:1, :]), rope(k0, gains[1:2, :]), v0.astype(jnp.bfloat16))
    rem = (rope(q1, gains[2:3, :]), rope(k1, gains[3:4, :]), v1.astype(jnp.bfloat16))
    at = pl.multiple_of(step * ROWS, ROWS)

    def store(kept, sent):
        for i in range(3):
            send[pl.ds(pl.multiple_of(1024 * i + at, ROWS), ROWS), :] = sent[i]

        @pl.when(step < 2)
        def _():
            keep_a[pl.ds(at, ROWS), :] = kept[0]

        @pl.when(step >= 2)
        def _():
            keep_b[pl.ds(pl.multiple_of(at - 512, ROWS), ROWS), :] = kept[0]

        keep_b[pl.ds(pl.multiple_of(512 + at, ROWS), ROWS), :] = kept[1]
        keep_b[pl.ds(pl.multiple_of(1536 + at, ROWS), ROWS), :] = kept[2]

    @pl.when(xl == xh)
    def _():
        store(loc, rem)

    @pl.when(xl != xh)
    def _():
        store(rem, loc)


def whole(a):
    return pl.BlockSpec(a.shape, lambda i, s: (0,) * a.ndim)


def rows_of(a):
    return pl.BlockSpec((a.shape[0], ROWS, 128), lambda i, s: (0, i, 0))


def project_near(idx, pieces, w_loc, w_own, w_oth):
    tok = pieces[0].shape[1]
    return pl.pallas_call(
        near_kernel,
        grid_spec=pltpu.PrefetchScalarGridSpec(
            num_scalar_prefetch=1,
            grid=(tok // ROWS,),
            in_specs=[rows_of(p) for p in pieces] + [whole(w_loc), whole(w_own), whole(w_oth)],
            out_specs=(
                pl.BlockSpec((ROWS, 768), lambda i, s: (i, 0)),
                pl.BlockSpec((1024, 768), lambda i, s: (0, 0)),
            ),
            scratch_shapes=[pltpu.VMEM((3072, 768), jnp.bfloat16)],
        ),
        out_shape=(
            jax.ShapeDtypeStruct((tok, 768), jnp.float32),
            jax.ShapeDtypeStruct((1024, 768), jnp.bfloat16),
        ),
        compiler_params=pltpu.CompilerParams(
            dimension_semantics=("arbitrary",), vmem_limit_bytes=40 * 1024 * 1024
        ),
        name="project_near",
    )(idx, *pieces, w_loc, w_own, w_oth)


def project_far(idx, pieces, acc, w_far, gains, cosine, sine):
    tok = pieces[0].shape[1]
    table = pl.BlockSpec((ROWS, 128), lambda i, s: (i, 0))
    out = (
        jax.ShapeDtypeStruct((tok // 2, 128), jnp.bfloat16),
        jax.ShapeDtypeStruct((5 * tok // 2, 128), jnp.bfloat16),
        jax.ShapeDtypeStruct((3 * tok, 128), jnp.bfloat16),
        jax.ShapeDtypeStruct((2, tok), jnp.float32),
    )
    return pl.pallas_call(
        far_kernel,
        grid_spec=pltpu.PrefetchScalarGridSpec(
            num_scalar_prefetch=1,
            grid=(tok // ROWS,),
            in_specs=[rows_of(p) for p in pieces]
            + [pl.BlockSpec((ROWS, 768), lambda i, s: (i, 0))]
            + [whole(w_far), whole(gains), table, table],
            out_specs=(whole(out[0]), whole(out[1]), whole(out[2]), pl.BlockSpec((2, ROWS), lambda i, s: (0, i))),
        ),
        out_shape=out,
        compiler_params=pltpu.CompilerParams(
            dimension_semantics=("arbitrary",), vmem_limit_bytes=40 * 1024 * 1024
        ),
        name="project_far",
    )(idx, *pieces, acc, w_far, gains, cosine, sine)


def attend_kernel(idx, keep_a, keep_b, recv, d_own, d_recv, near, other, out, peak, kbuf, vbuf, qbuf, sbuf, ksbuf):
    xl, c = idx[3], idx[4]
    tok = 1024
    vbuf[:, 128:] = jnp.ones((4096, 128), jnp.bfloat16)
    pieces = (
        (xl, c, keep_a, 0, keep_b, 512, 0, near, 0),
        (1 - xl, c, recv, 0, recv, 1024, 0, near, 1),
        (xl, 1 - c, d_own, 0, d_own, 512, 512, other, 0),
        (1 - xl, 1 - c, d_recv, 0, d_recv, 512, 512, other, 1),
    )
    for lo, co, q_ref, q_at, kv_ref, k_at, half, scales, at in pieces:
        quarter = lo * 2 + co
        base = pl.multiple_of(quarter * tok, tok)
        kbuf[pl.ds(base, tok), :] = kv_ref[k_at : k_at + tok, :]
        vbuf[pl.ds(base, tok), :128] = kv_ref[k_at + tok : k_at + 2 * tok, :]
        for i in range(2):
            ksbuf[pl.ds(2 * quarter + i, 1), :] = scales[at, 1:2, QB * i : QB * (i + 1)]
        scale = scales[at, 0:1, half : half + QB] * (128 ** (-0.5) * LOG2E)
        q = q_ref[q_at : q_at + QB, :].astype(jnp.float32) * jnp.broadcast_to(scale, (128, QB)).T
        qbuf[pl.ds(pl.multiple_of(quarter * QB, QB), QB), :] = q.astype(jnp.bfloat16)

    best = jnp.full((1, 1), NEG, jnp.float32)
    row = lax.broadcasted_iota(jnp.int32, (QB, QB), 0)
    col = lax.broadcasted_iota(jnp.int32, (QB, QB), 1)
    causal = col <= row
    for quarter in range(4):
        block = 2 * quarter + jnp.where(c == quarter % 2, 0, 1)
        q = qbuf[quarter * QB : (quarter + 1) * QB, :]

        def score(j, top, masked, q=q):
            at = pl.ds(pl.multiple_of(j * QB, QB), QB)
            s = lax.dot_general(q, kbuf[at, :], (((1,), (1,)), ((), ())), preferred_element_type=jnp.float32)
            s = s * ksbuf[pl.ds(j, 1), :]
            if masked:
                s = jnp.where(causal, s, NEG)
            sbuf[j] = s
            for i in range(QB // 128):
                top = jnp.maximum(top, s[:, 128 * i : 128 * (i + 1)])
            return top

        top = score(block, jnp.full((QB, 128), NEG, jnp.float32), True)
        top = lax.fori_loop(0, block, lambda j, t: score(j, t, False), top)
        top = jnp.max(top, axis=1, keepdims=True)

        def mix(j, accum, top=top):
            at = pl.ds(pl.multiple_of(j * QB, QB), QB)
            w = jnp.exp2(sbuf[j] - top).astype(jnp.bfloat16)
            return accum + jnp.dot(w, vbuf[at, :], preferred_element_type=jnp.float32)

        accum = lax.fori_loop(0, block + 1, mix, jnp.zeros((QB, 256), jnp.float32))
        out[quarter] = (accum[:, :128] / accum[:, 128:]).astype(jnp.bfloat16)
        best = jnp.maximum(best, jnp.max(top, axis=0, keepdims=True))
    peak[...] = jnp.broadcast_to(best, peak.shape)


def attend(idx, *args):
    return pl.pallas_call(
        attend_kernel,
        grid_spec=pltpu.PrefetchScalarGridSpec(
            num_scalar_prefetch=1,
            grid=(1,),
            in_specs=[whole(a) for a in args],
            out_specs=(
                pl.BlockSpec((4, QB, 128), lambda i, s: (0, 0, 0)),
                pl.BlockSpec((8, 128), lambda i, s: (0, 0)),
            ),
            scratch_shapes=[
                pltpu.VMEM((4096, 128), jnp.bfloat16),
                pltpu.VMEM((4096, 256), jnp.bfloat16),
                pltpu.VMEM((2048, 128), jnp.bfloat16),
                pltpu.VMEM((8, QB, QB), jnp.float32),
                pltpu.VMEM((8, QB), jnp.float32),
            ],
        ),
        out_shape=(
            jax.ShapeDtypeStruct((4, QB, 128), jnp.bfloat16),
            jax.ShapeDtypeStruct((8, 128), jnp.float32),
        ),
        compiler_params=pltpu.CompilerParams(vmem_limit_bytes=50 * 1024 * 1024),
        name="attend",
    )(idx, *args)


def out_kernel(idx, x, *refs):
    mine, other, out, xbuf = refs[:4], refs[4:8], refs[8], refs[9]
    z, xh, c = idx[0], idx[2], idx[4]
    step = pl.program_id(0)

    @pl.when(step == 0)
    def _():
        for i, d in enumerate((0, 3, 1, 2)):
            zz = (z + d) % 4
            for j in range(2):
                head = xh if j == 0 else 1 - xh
                for k in range(2):
                    xbuf[128 * k : 128 * k + 128, (2 * i + j) * 128 : (2 * i + j + 1) * 128] = x[head, k, zz]

    def emit(ws):
        w = jnp.concatenate([r[j] for r in ws for j in range(2)], axis=0)
        part = jnp.dot(xbuf[...], w, preferred_element_type=jnp.float32).astype(jnp.bfloat16)
        for i in range(4):
            out[i] = part[:, 128 * i : 128 * (i + 1)]

    @pl.when(step // 4 == c)
    def _():
        emit(mine)

    @pl.when(step // 4 != c)
    def _():
        emit(other)


def out_project(idx, x, mine, other):
    def columns(which):
        return pl.BlockSpec((2, 128, 512), lambda i, s: (0, 0, jnp.clip(i - 4 * which(s[4]), 0, 3)))

    return pl.pallas_call(
        out_kernel,
        grid_spec=pltpu.PrefetchScalarGridSpec(
            num_scalar_prefetch=1,
            grid=(8,),
            in_specs=[whole(x)] + [columns(lambda c: c)] * 4 + [columns(lambda c: 1 - c)] * 4,
            out_specs=pl.BlockSpec((4, 256, 128), lambda i, s: (i, 0, 0)),
            scratch_shapes=[pltpu.VMEM((256, 1024), jnp.bfloat16)],
        ),
        out_shape=jax.ShapeDtypeStruct((32, 256, 128), jnp.bfloat16),
        compiler_params=pltpu.CompilerParams(
            dimension_semantics=("arbitrary",), vmem_limit_bytes=40 * 1024 * 1024
        ),
        name="out_project",
    )(idx, x, *mine, *other)


def rope_tables(positions, head):
    half = head // 2
    freq = ROPE_BASE ** (-(jnp.arange(half, dtype=jnp.float32) * 2.0) / head)
    angle = positions[:, None] * freq[None, :]
    cosine, sine = jnp.cos(angle), jnp.sin(angle)
    return jnp.concatenate([cosine, cosine], 1), jnp.concatenate([-sine, sine], 1)


def layer(tokens, w_qkv, q_gain, k_gain, w_out):
    seqs, tok, head = tokens.shape
    width = w_qkv.shape[0]
    half = width // 2
    xl, c, z, y, xh = (lax.axis_index(a) for a in AXES)
    idx = jnp.stack([z, y, xh, xl, c]).astype(jnp.int32)

    mine = lax.dynamic_index_in_dim(tokens, xh, 0, keepdims=False)
    theirs = swap(lax.dynamic_index_in_dim(tokens, 1 - xh, 0, keepdims=False), "xh")

    w_loc = w_qkv.transpose(1, 0, 2)
    w_own = lax.ppermute(lax.dynamic_slice_in_dim(w_loc, c * half, half, 1), ("xl", "xh"), CROSS)
    gains = jnp.stack([q_gain, k_gain])
    gains = jnp.concatenate([gains, swap(gains, "xh")], 0)

    near_a, far_a = ring_relay(mine, *ring_direct(mine, "z"), "y")
    near_b, far_b = ring_relay(theirs, *ring_direct(theirs, "y"), "z")

    w_own, *_ = lax.optimization_barrier((w_own, near_a[2], near_a[5], near_b[2], near_b[5]))
    w_oth = swap(w_own, "c")

    positions = ((xl * 2 + c) * tok + jnp.arange(tok, dtype=jnp.int32)).astype(jnp.float32)
    cosine, sine = rope_tables(positions, head)
    acc, w_near_far = project_near(idx, near_a + near_b, w_loc, w_own, w_oth)

    keep_a, keep_b, send, ssq = project_far(
        idx, (*far_a, *far_b), acc, w_near_far, gains, cosine, sine
    )

    recv = swap(send, "xl")
    d_own = swap(keep_b, "c")

    ssq = to_all(ssq[None], ("z", "y")).sum(axis=0)
    inverse = lax.rsqrt(ssq / width + EPS)

    w_half = lax.dynamic_slice_in_dim(w_out, c * half, half, 1)
    w_pair = jnp.stack([w_half, lax.ppermute(w_half, ("xl", "xh"), CROSS)])
    w_pair, inverse = lax.optimization_barrier((w_pair, inverse))
    w_before = permute(w_pair, "z", 1)
    w_after = permute(w_pair, "z", -1)
    w_far = permute(w_pair, "z", 2)

    near = jnp.stack([inverse, swap(inverse, "xl")])
    other = swap(near, "c")
    partner = swap(inverse, "xh")
    low, high = jnp.where(xh == 0, inverse, partner), jnp.where(xh == 0, partner, inverse)
    qk_scale = jnp.stack([low, high], axis=1)

    d_recv = swap(recv[tok // 2 :], "c")

    attended, top = attend(idx, keep_a, keep_b, recv, d_own, d_recv, near, other)

    attended, w_before, w_after, w_far = lax.optimization_barrier((attended, w_before, w_after, w_far))
    w_mine = (w_pair, w_before, w_after, w_far)
    w_other = tuple(swap(w, "c") for w in w_mine)

    attended = attended.reshape(16, 128, 128)
    attended = lax.all_to_all(attended, ("xl", "c", "z"), 0, 0, tiled=True)
    partial_out = out_project(idx, attended.reshape(2, 2, 4, 128, 128), w_mine, w_other)
    pieces = lax.all_to_all(partial_out, TENSOR, 0, 0, tiled=True)
    pieces = pieces.reshape(4, 4, 2, 2, 128, 128).astype(jnp.float32).sum(axis=1)
    pieces = jnp.where(c == 0, pieces, pieces[:, :, ::-1])
    mixed = pieces.transpose(1, 2, 0, 3, 4).reshape(seqs, tok, head).astype(jnp.bfloat16)
    tops = to_all(top[:1] * (1.0 / LOG2E), ("xl", "c", "xh")).reshape(2, 2, 2, 128)
    peak = lax.dynamic_index_in_dim(tops, xh, 0, keepdims=False).max(axis=(0, 1))[:1]
    return (mixed, peak, qk_scale)


def solution(mesh):
    finer = Mesh(mesh.devices.reshape(2, 2, 4, 4, 2), AXES)
    seq = ("xl", "c")
    placed = (P(None, seq, TENSOR), P(None, None, TENSOR), P(TENSOR), P(TENSOR), P(TENSOR, None))
    return jax.shard_map(
        layer,
        mesh=finer,
        in_specs=placed,
        out_specs=(P(None, seq, TENSOR), P(TENSOR), P(None, None, seq)),
        check_vma=False,
    )
```

time: 594 us -> 231 us (0.39)
  waiting for transfers between devices: 488 us -> 94.5 us
  starting transfers between devices: 5.81 us -> 72.5 us
  matrix products: 43.7 us -> 0 us
  Pallas kernels: 0 us -> 41.1 us
  between operations: 14 us -> 0.95 us
  local copies, waits for them, and re-layouts: 18.1 us -> 10.6 us
  other arithmetic: 17.4 us -> 10 us
  blocking collectives: 6.36 us -> 0 us
    all_gather x2 -> x0, waiting for transfers between devices: 253 us -> none  [the longest x1 205 us: shards(): lax.all_gather(tokens, TENSOR, axis=2, tiled=True).reshape(rows, width)]
    reduce_scatter x2 -> x0, waiting for transfers between devices: 218 us -> none  [sum_by_axis(): array = lax.psum_scatter(array, axis, scatter_dimension=dim, tiled=True)]
    ppermute x0 -> x36, waiting for transfers between devices: none -> 76.3 us  [the longest x21 42.9 us: permute(): return lax.ppermute(array, axis, shift(4, k))]
    ppermute x0 -> x36, starting transfers between devices: none -> 53 us  [the longest x21 29.2 us: permute(): return lax.ppermute(array, axis, shift(4, k))]
    dot_general x7 -> x0, matrix products: 43.7 us -> none  [the longest x1 11.3 us: shards(): jnp.dot(whole, flat_w[:, 2 * dloc:], preferred_element_type=jnp.float32)]
    pallas_call x0 -> x4, Pallas kernels: none -> 41.1 us  [the longest x1 13.7 us: attend(): pl.pallas_call(attend_kernel, grid_spec=pltpu.PrefetchScalarGridSpec(num_...]
    all_to_all x1 -> x4, waiting for transfers between devices: 0.52 us -> 18.2 us  [the longest x1 10.2 us: layer(): attended = lax.all_to_all(attended, ('xl', 'c', 'z'), 0, 0, tiled=True)]
    unnamed x6 -> x0, waiting for transfers between devices: 16.1 us -> none
  transfers between devices with their start and end apart: 6 -> 40, of which waited for: 6 -> 17; matrix products, arithmetic and copies ran while one was open for 4% -> 6% of each run, Pallas kernels for 0% -> 18%
where the time goes in v1:
time: 231 us; the launch traced here: 230 us
  waiting for transfers between devices  94.5 us (41%)
  starting transfers between devices  72.5 us (31%)
  Pallas kernels  41.1 us (18%)
  local copies, waits for them, and re-layouts  10.6 us (5%)
  other arithmetic  10 us (4%)
    ppermute x21, waiting for transfers between devices, permute(): return lax.ppermute(array, axis, shift(4, k))  42.9 us
    ppermute x13, waiting for transfers between devices, swap(): return lax.ppermute(array, axis, [(0, 1), (1, 0)])  33.4 us
    ppermute x21, starting transfers between devices, permute(): return lax.ppermute(array, axis, shift(4, k))  29.2 us
    ppermute x13, starting transfers between devices, swap(): return lax.ppermute(array, axis, [(0, 1), (1, 0)])  20.3 us
    pallas_call x1, Pallas kernels, attend(): pl.pallas_call(attend_kernel, grid_spec=pltpu.PrefetchScalarGridSpec(num_...  13.7 us
    pallas_call x1, Pallas kernels, project_near(): pl.pallas_call(near_kernel, grid_spec=pltpu.PrefetchScalarGridSpec(num_sc...  12.2 us
    all_to_all x1, waiting for transfers between devices, layer(): attended = lax.all_to_all(attended, ('xl', 'c', 'z'), 0, 0, tiled=True)  10.2 us
    all_to_all x2, starting transfers between devices, to_all(): lax.all_to_all(jnp.broadcast_to(array, (size, *array.shape[1:])), axes, 0...  9.56 us
  transfers between devices with their start and end apart: 40, of which 17 were waited for; matrix products, arithmetic and copies ran while one was open for 6% of the time, Pallas kernels for 18%

profile of v1, /device:TPU:1, one launch (start us, length us, event | category | flops | bytes accessed | tf_op | source)
XLA Modules:
  0.0 229.7 jit_solution(7608955863351689285)
XLA Ops:
  3.4 3.3 %collective-permute-start.19 = (bf16[3,2048,128]{2,1,0:T(8,128)(2,1)}, bf16[3,2048,128]{2,1,0:T(8,128)(2,1)}, u32[]{:S(2)}, u32[]{:S(2)}) collective-permute-start(bf16[3,2048,128]{2,1,0:T(8,128)(2,1)} %dynamic-slice_bitcast_fusion), channel_id=1, source_target_pairs={{0,65},{65,0},{1,64},{64,1},{2,67},{67,2},{3,66},{66,3},{4,69},{69... | collective-permute-start | bytes 4718600 | tf_op jit(solution)/shard_map/ppermute | solution.py:368
  7.4 3.8 %collective-permute-start.3 = (bf16[1024,128]{1,0:T(8,128)(2,1)S(1)}, bf16[1024,128]{1,0:T(8,128)(2,1)S(1)}, u32[]{:S(2)}, u32[]{:S(2)}) collective-permute-start(bf16[1024,128]{1,0:T(8,128)(2,1)S(1)} %bitcast.44), channel_id=1, source_target_pairs={{0,24},{8,0},{16,8},{24,16},{1,25},{9,1},{17,9},{25,17},{2,26},{10... | collective-permute-start | bytes 786440 | tf_op jit(solution)/shard_map/ppermute | solution.py:37
  11.8 3.5 %collective-permute-done.7 = bf16[1024,128]{1,0:T(8,128)(2,1)S(1)} collective-permute-done((bf16[1024,128]{1,0:T(8,128)(2,1)S(1)}, bf16[1024,128]{1,0:T(8,128)(2,1)S(1)}, u32[]{:S(2)}, u32[]{:S(2)}) %collective-permute-start.7) | collective-permute-done | bytes 262176 | tf_op jit(solution)/shard_map/ppermute | solution.py:28
  29.0 3.2 %collective-permute-start.13 = (bf16[2,1024,128]{2,1,0:T(8,128)(2,1)S(1)}, bf16[2,1024,128]{2,1,0:T(8,128)(2,1)S(1)}, u32[]{:S(2)}, u32[]{:S(2)}) collective-permute-start(bf16[2,1024,128]{2,1,0:T(8,128)(2,1)S(1)} %pad_maximum_fusion.4.refs_7_), channel_id=1, source_target_pairs={{0,24},{8,0},{16,8},{24,16},{1,25},{9,1},{17,9},{25,17},{2,26},{10... | collective-permute-start | bytes 1572872 | tf_op jit(solution)/shard_map/ppermute | solution.py:37
  35.4 6.2 %collective-permute-done.5.refs_5_ = bf16[2,1024,128]{2,1,0:T(8,128)(2,1)S(1)} collective-permute-done((bf16[2,1024,128]{2,1,0:T(8,128)(2,1)S(1)}, bf16[2,1024,128]{2,1,0:T(8,128)(2,1)S(1)}, u32[]{:S(2)}, u32[]{:S(2)}) %collective-permute-start.5) | collective-permute-done | bytes 524320 | tf_op jit(solution)/shard_map/ppermute | solution.py:37
  41.6 4.9 %collective-permute-done.1.refs_2_ = bf16[2,1024,128]{2,1,0:T(8,128)(2,1)S(1)} collective-permute-done((bf16[2,1024,128]{2,1,0:T(8,128)(2,1)S(1)}, bf16[2,1024,128]{2,1,0:T(8,128)(2,1)S(1)}, u32[]{:S(2)}, u32[]{:S(2)}) %collective-permute-start.1) | collective-permute-done | bytes 524320 | tf_op jit(solution)/shard_map/ppermute | solution.py:37
  49.3 3.6 %collective-permute-start.20 = (bf16[3,2048,128]{2,1,0:T(8,128)(2,1)}, bf16[3,2048,128]{2,1,0:T(8,128)(2,1)}, u32[]{:S(2)}, u32[]{:S(2)}) collective-permute-start(bf16[3,2048,128]{2,1,0:T(8,128)(2,1)} %collective-permute-done.19.refs_13_), channel_id=1, source_target_pairs={{0,32},{32,0},{1,33},{33,1},{2,34},{34,2},{3,35},{35,3},{4,36},{36... | collective-permute-start | bytes 4718600 | tf_op jit(solution)/shard_map/ppermute | solution.py:28
  61.5 8.2 %collective-permute-done.15.refs_3_ = bf16[2,1024,128]{2,1,0:T(8,128)(2,1)} collective-permute-done((bf16[2,1024,128]{2,1,0:T(8,128)(2,1)S(1)}, bf16[2,1024,128]{2,1,0:T(8,128)(2,1)}, u32[]{:S(2)}, u32[]{:S(2)}) %collective-permute-start.15) | collective-permute-done | bytes 524320 | tf_op jit(solution)/shard_map/ppermute | solution.py:37
  74.3 3.2 %fusion.2 = (f32[1024,64]{1,0:T(8,128)}, f32[1024,64]{1,0:T(8,128)}, f32[1024,64]{1,0:T(8,128)}) fusion(f32[64]{0:T(128)S(1)} %multiply_power_fusion, f32[1024]{0:T(1024)S(1)} %add_convert_fusion), kind=kLoop, calls=%fused_computation.15 | loop fusion | flops 131072 | bytes 790784 | tf_op jit(solution)/shard_map/neg | solution.py:354
  80.5 12.2 %project_near.1 = (f32[1024,768]{1,0:T(8,128)S(1)}, bf16[1024,768]{1,0:T(8,128)(2,1)S(1)}) custom-call(s32[5]{0:T(128)S(1)} %stack.93.idx, bf16[2,1024,128]{2,1,0:T(8,128)(2,1)S(1)} %pad_maximum_fusion.1.refs_0_, bf16[2,1024,128]{2,1,0:T(8,128)(2,1)S(1)} %pad_maximum_fusion.2.refs_1_, bf16[2,1024,128]{2,1,0:T(8,128)(2,1)S(1)} %copy-done.4, ...), custom_call_target="tpu_custom_call" | custom-call | tf_op jit(solution)/shard_map/project_near/pallas_call | solution.py:166
  92.7 6.1 %project_far.1 = (bf16[512,128]{1,0:T(8,128)(2,1)S(1)}, bf16[2560,128]{1,0:T(8,128)(2,1)S(1)}, bf16[3072,128]{1,0:T(8,128)(2,1)}, f32[2,1024]{1,0:T(2,128)S(1)}) custom-call(s32[5]{0:T(128)S(1)} %stack.93.idx, bf16[2,1024,128]{2,1,0:T(8,128)(2,1)} %collective-permute-done.2.refs_0_, bf16[2,1024,128]{2,1,0:T(8,128)(2,1)} %collective-permute-done.6.refs_1_, ...), custom_call_target="tpu_custom_call" | custom-call | tf_op jit(solution)/shard_map/project_far/pallas_call | solution.py:198
  100.1 5.7 %all-to-all-start = ((f32[16,2,1024]{2,1,0:T(2,128)}), f32[16,2,1024]{2,1,0:T(2,128)}, u32[]{:S(2)}, u32[]{:S(2)}) async-start(f32[16,2,1024]{2,1,0:T(2,128)} %broadcast_in_dim.4), calls=%async_computation | async-start | bytes 262144 | tf_op jit(solution)/shard_map/all_to_all | solution.py:33
  107.5 5.2 %all-to-all-done = f32[16,2,1024]{2,1,0:T(2,128)} async-done(((f32[16,2,1024]{2,1,0:T(2,128)}), f32[16,2,1024]{2,1,0:T(2,128)}, u32[]{:S(2)}, u32[]{:S(2)}) %all-to-all-start) | async-done | bytes 131104 | tf_op jit(solution)/shard_map/all_to_all | solution.py:33
  118.0 4.7 %collective-permute-done.26 = f32[2,1024]{1,0:T(2,128)S(1)} collective-permute-done((f32[2,1024]{1,0:T(2,128)S(1)}, f32[2,1024]{1,0:T(2,128)S(1)}, u32[]{:S(2)}, u32[]{:S(2)}) %collective-permute-start.26) | collective-permute-done | bytes 8224 | tf_op jit(solution)/shard_map/ppermute | solution.py:28
  122.7 3.7 %collective-permute-start.27 = (f32[2,2,1024]{2,1,0:T(2,128)S(1)}, f32[2,2,1024]{2,1,0:T(2,128)S(1)}, u32[]{:S(2)}, u32[]{:S(2)}) collective-permute-start(f32[2,2,1024]{2,1,0:T(2,128)S(1)} %pad_maximum_fusion.7.near), channel_id=1, source_target_pairs={{0,32},{32,0},{1,33},{33,1},{2,34},{34,2},{3,35},{35,3},{4,36},{36... | collective-permute-start | bytes 49160 | tf_op jit(solution)/shard_map/ppermute | solution.py:28
  130.3 13.7 %attend.1 = (bf16[4,512,128]{2,1,0:T(8,128)(2,1)S(1)}, f32[8,128]{1,0:T(8,128)S(1)}) custom-call(s32[5]{0:T(128)S(1)} %stack.93.idx, bf16[512,128]{1,0:T(8,128)(2,1)S(1)} %copy-done.11, bf16[2560,128]{1,0:T(8,128)(2,1)S(1)} %get-tuple-element.22.keep_b, bf16[3072,128]{1,0:T(8,128)(2,1)S(1)} %collective-permute-done.22.recv, ...), custom_call_target="tpu_custom_call" | custom-call | tf_op jit(solution)/shard_map/attend/pallas_call | solution.py:272
  144.8 13.9 %collective-permute-done.30.refs_3_ = bf16[2,128,2048]{2,1,0:T(8,128)(2,1)} collective-permute-done((bf16[2,128,2048]{2,1,0:T(8,128)(2,1)S(1)}, bf16[2,128,2048]{2,1,0:T(8,128)(2,1)}, u32[]{:S(2)}, u32[]{:S(2)}) %collective-permute-start.30) | collective-permute-done | bytes 1048608 | tf_op jit(solution)/shard_map/ppermute | solution.py:37
  158.8 5.7 %collective-permute-start.32 = (bf16[2,128,2048]{2,1,0:T(8,128)(2,1)}, bf16[2,128,2048]{2,1,0:T(8,128)(2,1)}, u32[]{:S(2)}, u32[]{:S(2)}) collective-permute-start(bf16[2,128,2048]{2,1,0:T(8,128)(2,1)} %collective-permute-done.28.refs_1_), channel_id=1, source_target_pairs={{0,32},{32,0},{1,33},{33,1},{2,34},{34,2},{3,35},{35,3},{4,36},{36... | collective-permute-start | bytes 3145736 | tf_op jit(solution)/shard_map/ppermute | solution.py:28
  164.9 4.4 %all-to-all-start.1 = ((bf16[16,128,128]{2,1,0:T(8,128)(2,1)}), bf16[16,128,128]{2,1,0:T(8,128)(2,1)S(1)}, u32[]{:S(2)}, u32[]{:S(2)}) async-start(bf16[16,128,128]{2,1,0:T(8,128)(2,1)} %bitcast.41), calls=%async_computation.1 | async-start | bytes 1048576 | tf_op jit(solution)/shard_map/all_to_all | solution.py:414
  169.3 10.2 %all-to-all-done.1 = bf16[16,128,128]{2,1,0:T(8,128)(2,1)S(1)} async-done(((bf16[16,128,128]{2,1,0:T(8,128)(2,1)}), bf16[16,128,128]{2,1,0:T(8,128)(2,1)S(1)}, u32[]{:S(2)}, u32[]{:S(2)}) %all-to-all-start.1) | async-done | bytes 524320 | tf_op jit(solution)/shard_map/all_to_all | solution.py:414
  180.1 3.8 %all-to-all-start.3 = ((f32[8,1,128]{2,1,0:T(1,128)}), f32[8,1,128]{2,1,0:T(1,128)S(1)}, u32[]{:S(2)}, u32[]{:S(2)}) async-start(f32[8,1,128]{2,1,0:T(1,128)} %broadcast_in_dim.5), calls=%async_computation.3 | async-start | bytes 8192 | tf_op jit(solution)/shard_map/all_to_all | solution.py:33
  183.9 9.1 %out_project.1 = bf16[32,256,128]{2,1,0:T(8,128)(2,1)} custom-call(s32[5]{0:T(128)S(1)} %stack.93.idx, bf16[2,2,4,128,128]{4,3,2,1,0:T(8,128)(2,1)S(1)} %bitcast.40, bf16[2,128,2048]{2,1,0:T(8,128)(2,1)S(1)} %pad_maximum_fusion.refs_0_, bf16[2,128,2048]{2,1,0:T(8,128)(2,1)} %collective-permute-done.28.refs_1_, ...), custom_call_target="tpu_custom_call" | custom-call | tf_op jit(solution)/shard_map/out_project/pallas_call | solution.py:332
  193.0 5.6 %all-to-all-start.2 = ((bf16[32,256,128]{2,1,0:T(8,128)(2,1)}), bf16[32,256,128]{2,1,0:T(8,128)(2,1)S(1)}, u32[]{:S(2)}, u32[]{:S(2)}) async-start(bf16[32,256,128]{2,1,0:T(8,128)(2,1)} %out_project.1), calls=%async_computation.2 | async-start | bytes 4194304 | tf_op jit(solution)/shard_map/all_to_all | solution.py:416
  201.5 22.8 %collective-permute-done.35 = f32[2,1024]{1,0:T(2,128)S(1)} collective-permute-done((f32[2,1024]{1,0:T(2,128)S(1)}, f32[2,1024]{1,0:T(2,128)S(1)}, u32[]{:S(2)}, u32[]{:S(2)}) %collective-permute-start.35) | collective-permute-done | bytes 8224 | tf_op jit(solution)/shard_map/ppermute | solution.py:28
  (120 shorter events, 62.0 us)
Async XLA Ops:
  3.4 45.9 %collective-permute-start.19 = (bf16[3,2048,128]{2,1,0:T(8,128)(2,1)}, bf16[3,2048,128]{2,1,0:T(8,128)(2,1)}, u32[]{:S(2)}, u32[]{:S(2)}) collective-permute-start(bf16[3,2048,128]{2,1,0:T(8,128)(2,1)} %dynamic-slice_bitcast_fusion), channel_id=1, source_target_pairs={{0,65},{65,0},{1,64},{64,1},{2,67},{67,2},{3,66},{66,3},{4,69},{69... | collective-permute-start | bytes 4718600 | tf_op jit(solution)/shard_map/ppermute | solution.py:368
  11.1 14.9 %collective-permute-start = (bf16[1024,128]{1,0:T(8,128)(2,1)S(1)}, bf16[1024,128]{1,0:T(8,128)(2,1)S(1)}, u32[]{:S(2)}, u32[]{:S(2)}) collective-permute-start(bf16[1024,128]{1,0:T(8,128)(2,1)S(1)} %bitcast.46), channel_id=1, source_target_pairs={{0,8},{8,16},{16,24},{24,0},{1,9},{9,17},{17,25},{25,1},{2,10},{10... | collective-permute-start | bytes 786440 | tf_op jit(solution)/shard_map/ppermute | solution.py:37
  26.0 15.5 %collective-permute-start.5 = (bf16[2,1024,128]{2,1,0:T(8,128)(2,1)S(1)}, bf16[2,1024,128]{2,1,0:T(8,128)(2,1)S(1)}, u32[]{:S(2)}, u32[]{:S(2)}) collective-permute-start(bf16[2,1024,128]{2,1,0:T(8,128)(2,1)S(1)} %pad_maximum_fusion.2.refs_1_), channel_id=1, source_target_pairs={{0,6},{2,0},{4,2},{6,4},{1,7},{3,1},{5,3},{7,5},{8,14},{10,8},{12,... | collective-permute-start | bytes 1572872 | tf_op jit(solution)/shard_map/ppermute | solution.py:37
  28.8 17.7 %collective-permute-start.1 = (bf16[2,1024,128]{2,1,0:T(8,128)(2,1)S(1)}, bf16[2,1024,128]{2,1,0:T(8,128)(2,1)S(1)}, u32[]{:S(2)}, u32[]{:S(2)}) collective-permute-start(bf16[2,1024,128]{2,1,0:T(8,128)(2,1)S(1)} %pad_maximum_fusion.1.refs_0_), channel_id=1, source_target_pairs={{0,2},{2,4},{4,6},{6,0},{1,3},{3,5},{5,7},{7,1},{8,10},{10,12},{12... | collective-permute-start | bytes 1572872 | tf_op jit(solution)/shard_map/ppermute | solution.py:37
  29.0 17.5 %collective-permute-start.13 = (bf16[2,1024,128]{2,1,0:T(8,128)(2,1)S(1)}, bf16[2,1024,128]{2,1,0:T(8,128)(2,1)S(1)}, u32[]{:S(2)}, u32[]{:S(2)}) collective-permute-start(bf16[2,1024,128]{2,1,0:T(8,128)(2,1)S(1)} %pad_maximum_fusion.4.refs_7_), channel_id=1, source_target_pairs={{0,24},{8,0},{16,8},{24,16},{1,25},{9,1},{17,9},{25,17},{2,26},{10... | collective-permute-start | bytes 1572872 | tf_op jit(solution)/shard_map/ppermute | solution.py:37
  49.3 25.0 %collective-permute-start.20 = (bf16[3,2048,128]{2,1,0:T(8,128)(2,1)}, bf16[3,2048,128]{2,1,0:T(8,128)(2,1)}, u32[]{:S(2)}, u32[]{:S(2)}) collective-permute-start(bf16[3,2048,128]{2,1,0:T(8,128)(2,1)} %collective-permute-done.19.refs_13_), channel_id=1, source_target_pairs={{0,32},{32,0},{1,33},{33,1},{2,34},{34,2},{3,35},{35,3},{4,36},{36... | collective-permute-start | bytes 4718600 | tf_op jit(solution)/shard_map/ppermute | solution.py:28
  55.2 14.5 %collective-permute-start.15 = (bf16[2,1024,128]{2,1,0:T(8,128)(2,1)S(1)}, bf16[2,1024,128]{2,1,0:T(8,128)(2,1)}, u32[]{:S(2)}, u32[]{:S(2)}) collective-permute-start(bf16[2,1024,128]{2,1,0:T(8,128)(2,1)S(1)} %pad_maximum_fusion.2.refs_1_), channel_id=1, source_target_pairs={{0,2},{2,4},{4,6},{6,0},{1,3},{3,5},{5,7},{7,1},{8,10},{10,12},{12... | collective-permute-start | bytes 1572872 | tf_op jit(solution)/shard_map/ppermute | solution.py:37
  55.4 14.4 %collective-permute-start.16 = (bf16[2,1024,128]{2,1,0:T(8,128)(2,1)S(1)}, bf16[2,1024,128]{2,1,0:T(8,128)(2,1)}, u32[]{:S(2)}, u32[]{:S(2)}) collective-permute-start(bf16[2,1024,128]{2,1,0:T(8,128)(2,1)S(1)} %pad_maximum_fusion.1.refs_0_), channel_id=1, source_target_pairs={{0,6},{2,0},{4,2},{6,4},{1,7},{3,1},{5,3},{7,5},{8,14},{10,8},{12,... | collective-permute-start | bytes 1572872 | tf_op jit(solution)/shard_map/ppermute | solution.py:37
  69.7 36.5 %collective-permute-start.25 = (bf16[128,2048]{1,0:T(8,128)(2,1)}, bf16[128,2048]{1,0:T(8,128)(2,1)}, u32[]{:S(2)}, u32[]{:S(2)}) collective-permute-start(bf16[128,2048]{1,0:T(8,128)(2,1)} %constant_dynamic-slice_fusion), channel_id=1, source_target_pairs={{0,65},{65,0},{1,64},{64,1},{2,67},{67,2},{3,66},{66,3},{4,69},{69... | collective-permute-start | bytes 1572872 | tf_op jit(solution)/shard_map/ppermute | solution.py:393
  69.9 22.7 %collective-permute-start.6 = (bf16[2,1024,128]{2,1,0:T(8,128)(2,1)}, bf16[2,1024,128]{2,1,0:T(8,128)(2,1)}, u32[]{:S(2)}, u32[]{:S(2)}) collective-permute-start(bf16[2,1024,128]{2,1,0:T(8,128)(2,1)} %copy-done.1), channel_id=1, source_target_pairs={{0,6},{2,0},{4,2},{6,4},{1,7},{3,1},{5,3},{7,5},{8,14},{10,8},{12,... | collective-permute-start | bytes 1572872 | tf_op jit(solution)/shard_map/ppermute | solution.py:37
  72.1 20.6 %collective-permute-start.2 = (bf16[2,1024,128]{2,1,0:T(8,128)(2,1)}, bf16[2,1024,128]{2,1,0:T(8,128)(2,1)}, u32[]{:S(2)}, u32[]{:S(2)}) collective-permute-start(bf16[2,1024,128]{2,1,0:T(8,128)(2,1)} %copy-done.3), channel_id=1, source_target_pairs={{0,2},{2,4},{4,6},{6,0},{1,3},{3,5},{5,7},{7,1},{8,10},{10,12},{12... | collective-permute-start | bytes 1572872 | tf_op jit(solution)/shard_map/ppermute | solution.py:37
  72.1 20.6 %collective-permute-start.14 = (bf16[2,1024,128]{2,1,0:T(8,128)(2,1)}, bf16[2,1024,128]{2,1,0:T(8,128)(2,1)}, u32[]{:S(2)}, u32[]{:S(2)}) collective-permute-start(bf16[2,1024,128]{2,1,0:T(8,128)(2,1)} %copy-done.5), channel_id=1, source_target_pairs={{0,24},{8,0},{16,8},{24,16},{1,25},{9,1},{17,9},{25,17},{2,26},{10... | collective-permute-start | bytes 1572872 | tf_op jit(solution)/shard_map/ppermute | solution.py:37
  74.3 18.4 %collective-permute-start.10 = (bf16[2,1024,128]{2,1,0:T(8,128)(2,1)}, bf16[2,1024,128]{2,1,0:T(8,128)(2,1)}, u32[]{:S(2)}, u32[]{:S(2)}) collective-permute-start(bf16[2,1024,128]{2,1,0:T(8,128)(2,1)} %copy-done.7), channel_id=1, source_target_pairs={{0,8},{8,16},{16,24},{24,0},{1,9},{9,17},{17,25},{25,1},{2,10},{10... | collective-permute-start | bytes 1572872 | tf_op jit(solution)/shard_map/ppermute | solution.py:37
  105.8 20.5 %collective-permute-start.22 = (bf16[3072,128]{1,0:T(8,128)(2,1)}, bf16[3072,128]{1,0:T(8,128)(2,1)S(1)}, u32[]{:S(2)}, u32[]{:S(2)}) collective-permute-start(bf16[3072,128]{1,0:T(8,128)(2,1)} %get-tuple-element.23), channel_id=1, source_target_pairs={{0,64},{64,0},{1,65},{65,1},{2,66},{66,2},{3,67},{67,3},{4,68},{68... | collective-permute-start | bytes 2359304 | tf_op jit(solution)/shard_map/ppermute | solution.py:28
  115.0 29.8 %collective-permute-start.28 = (bf16[2,128,2048]{2,1,0:T(8,128)(2,1)S(1)}, bf16[2,128,2048]{2,1,0:T(8,128)(2,1)}, u32[]{:S(2)}, u32[]{:S(2)}) collective-permute-start(bf16[2,128,2048]{2,1,0:T(8,128)(2,1)S(1)} %pad_maximum_fusion.refs_0_), channel_id=1, source_target_pairs={{0,8},{8,16},{16,24},{24,0},{1,9},{9,17},{17,25},{25,1},{2,10},{10... | collective-permute-start | bytes 3145736 | tf_op jit(solution)/shard_map/ppermute | solution.py:37
  115.1 29.7 %collective-permute-start.29 = (bf16[2,128,2048]{2,1,0:T(8,128)(2,1)S(1)}, bf16[2,128,2048]{2,1,0:T(8,128)(2,1)}, u32[]{:S(2)}, u32[]{:S(2)}) collective-permute-start(bf16[2,128,2048]{2,1,0:T(8,128)(2,1)S(1)} %pad_maximum_fusion.refs_0_), channel_id=1, source_target_pairs={{0,24},{8,0},{16,8},{24,16},{1,25},{9,1},{17,9},{25,17},{2,26},{10... | collective-permute-start | bytes 3145736 | tf_op jit(solution)/shard_map/ppermute | solution.py:37
  117.7 41.0 %collective-permute-start.30 = (bf16[2,128,2048]{2,1,0:T(8,128)(2,1)S(1)}, bf16[2,128,2048]{2,1,0:T(8,128)(2,1)}, u32[]{:S(2)}, u32[]{:S(2)}) collective-permute-start(bf16[2,128,2048]{2,1,0:T(8,128)(2,1)S(1)} %pad_maximum_fusion.refs_0_), channel_id=1, source_target_pairs={{0,16},{8,24},{16,0},{24,8},{1,17},{9,25},{17,1},{25,9},{2,18},{10... | collective-permute-start | bytes 3145736 | tf_op jit(solution)/shard_map/ppermute | solution.py:37
  128.4 55.4 %collective-permute-start.31 = (bf16[2,128,2048]{2,1,0:T(8,128)(2,1)S(1)}, bf16[2,128,2048]{2,1,0:T(8,128)(2,1)}, u32[]{:S(2)}, u32[]{:S(2)}) collective-permute-start(bf16[2,128,2048]{2,1,0:T(8,128)(2,1)S(1)} %pad_maximum_fusion.refs_0_), channel_id=1, source_target_pairs={{0,32},{32,0},{1,33},{33,1},{2,34},{34,2},{3,35},{35,3},{4,36},{36... | collective-permute-start | bytes 3145736 | tf_op jit(solution)/shard_map/ppermute | solution.py:28
  158.8 25.1 %collective-permute-start.32 = (bf16[2,128,2048]{2,1,0:T(8,128)(2,1)}, bf16[2,128,2048]{2,1,0:T(8,128)(2,1)}, u32[]{:S(2)}, u32[]{:S(2)}) collective-permute-start(bf16[2,128,2048]{2,1,0:T(8,128)(2,1)} %collective-permute-done.28.refs_1_), channel_id=1, source_target_pairs={{0,32},{32,0},{1,33},{33,1},{2,34},{34,2},{3,35},{35,3},{4,36},{36... | collective-permute-start | bytes 3145736 | tf_op jit(solution)/shard_map/ppermute | solution.py:28
  164.4 19.5 %collective-permute-start.33 = (bf16[2,128,2048]{2,1,0:T(8,128)(2,1)}, bf16[2,128,2048]{2,1,0:T(8,128)(2,1)}, u32[]{:S(2)}, u32[]{:S(2)}) collective-permute-start(bf16[2,128,2048]{2,1,0:T(8,128)(2,1)} %collective-permute-done.29.refs_2_), channel_id=1, source_target_pairs={{0,32},{32,0},{1,33},{33,1},{2,34},{34,2},{3,35},{35,3},{4,36},{36... | collective-permute-start | bytes 3145736 | tf_op jit(solution)/shard_map/ppermute | solution.py:28
  164.5 19.4 %collective-permute-start.34 = (bf16[2,128,2048]{2,1,0:T(8,128)(2,1)}, bf16[2,128,2048]{2,1,0:T(8,128)(2,1)}, u32[]{:S(2)}, u32[]{:S(2)}) collective-permute-start(bf16[2,128,2048]{2,1,0:T(8,128)(2,1)} %collective-permute-done.30.refs_3_), channel_id=1, source_target_pairs={{0,32},{32,0},{1,33},{33,1},{2,34},{34,2},{3,35},{35,3},{4,36},{36... | collective-permute-start | bytes 3145736 | tf_op jit(solution)/shard_map/ppermute | solution.py:28
  164.9 14.5 %all-to-all-start.1 = ((bf16[16,128,128]{2,1,0:T(8,128)(2,1)}), bf16[16,128,128]{2,1,0:T(8,128)(2,1)S(1)}, u32[]{:S(2)}, u32[]{:S(2)}) async-start(bf16[16,128,128]{2,1,0:T(8,128)(2,1)} %bitcast.41), calls=%async_computation.1 | async-start | bytes 1048576 | tf_op jit(solution)/shard_map/all_to_all | solution.py:414
  193.0 35.2 %all-to-all-start.2 = ((bf16[32,256,128]{2,1,0:T(8,128)(2,1)}), bf16[32,256,128]{2,1,0:T(8,128)(2,1)S(1)}, u32[]{:S(2)}, u32[]{:S(2)}) async-start(bf16[32,256,128]{2,1,0:T(8,128)(2,1)} %out_project.1), calls=%async_computation.2 | async-start | bytes 4194304 | tf_op jit(solution)/shard_map/all_to_all | solution.py:416
  198.7 25.7 %collective-permute-start.35 = (f32[2,1024]{1,0:T(2,128)S(1)}, f32[2,1024]{1,0:T(2,128)S(1)}, u32[]{:S(2)}, u32[]{:S(2)}) collective-permute-start(f32[2,1024]{1,0:T(2,128)S(1)} %add_rsqrt_fusion), channel_id=1, source_target_pairs={{0,1},{1,0},{2,3},{3,2},{4,5},{5,4},{6,7},{7,6},{8,9},{9,8},{10,11... | collective-permute-start | bytes 24584 | tf_op jit(solution)/shard_map/ppermute | solution.py:28
  (31 other events, 330.8 us)

commit v2 on v1

--- a/solution.py
+++ b/solution.py
@@ -17,6 +17,8 @@
 
 ROWS = 256
 QB = 512
+OUT_COLS = 1024
+OUT_STEPS = 2048 // OUT_COLS
 CROSS = [(0, 3), (3, 0), (1, 2), (2, 1)]
 
 
@@ -31,6 +33,11 @@
 def to_all(array, axes):
     size = lax.axis_size(axes)
     return lax.all_to_all(jnp.broadcast_to(array, (size, *array.shape[1:])), axes, 0, 0, tiled=True)
+
+
+def exchange(array, axes):
+    n = 2 ** len(axes)
+    return lax.ppermute(array, axes, [(i, n - 1 - i) for i in range(n)])
 
 
 def permute(array, axis, k):
@@ -213,24 +220,24 @@
     )(idx, *pieces, acc, w_far, gains, cosine, sine)
 
 
-def attend_kernel(idx, keep_a, keep_b, recv, d_own, d_recv, near, other, out, peak, kbuf, vbuf, qbuf, sbuf, ksbuf):
+def attend_kernel(idx, keep_a, keep_b, recv, d_own, d_recv, s0, s1, s2, s3, out, peak, kbuf, vbuf, qbuf, sbuf, ksbuf):
     xl, c = idx[3], idx[4]
     tok = 1024
     vbuf[:, 128:] = jnp.ones((4096, 128), jnp.bfloat16)
     pieces = (
-        (xl, c, keep_a, 0, keep_b, 512, 0, near, 0),
-        (1 - xl, c, recv, 0, recv, 1024, 0, near, 1),
-        (xl, 1 - c, d_own, 0, d_own, 512, 512, other, 0),
-        (1 - xl, 1 - c, d_recv, 0, d_recv, 512, 512, other, 1),
+        (xl, c, keep_a, 0, keep_b, 512, 0, s0),
+        (1 - xl, c, recv, 0, recv, 1024, 0, s1),
+        (xl, 1 - c, d_own, 0, d_own, 512, 512, s2),
+        (1 - xl, 1 - c, d_recv, 0, d_recv, 512, 512, s3),
     )
-    for lo, co, q_ref, q_at, kv_ref, k_at, half, scales, at in pieces:
+    for lo, co, q_ref, q_at, kv_ref, k_at, half, scales in pieces:
         quarter = lo * 2 + co
         base = pl.multiple_of(quarter * tok, tok)
         kbuf[pl.ds(base, tok), :] = kv_ref[k_at : k_at + tok, :]
         vbuf[pl.ds(base, tok), :128] = kv_ref[k_at + tok : k_at + 2 * tok, :]
         for i in range(2):
-            ksbuf[pl.ds(2 * quarter + i, 1), :] = scales[at, 1:2, QB * i : QB * (i + 1)]
-        scale = scales[at, 0:1, half : half + QB] * (128 ** (-0.5) * LOG2E)
+            ksbuf[pl.ds(2 * quarter + i, 1), :] = scales[1:2, QB * i : QB * (i + 1)]
+        scale = scales[0:1, half : half + QB] * (128 ** (-0.5) * LOG2E)
         q = q_ref[q_at : q_at + QB, :].astype(jnp.float32) * jnp.broadcast_to(scale, (128, QB)).T
         qbuf[pl.ds(pl.multiple_of(quarter * QB, QB), QB), :] = q.astype(jnp.bfloat16)
 
@@ -297,7 +304,7 @@
 
 
 def out_kernel(idx, x, *refs):
-    mine, other, out, xbuf = refs[:4], refs[4:8], refs[8], refs[9]
+    mine, other, out, xbuf = refs[:5], refs[5:10], refs[10], refs[11]
     z, xh, c = idx[0], idx[2], idx[4]
     step = pl.program_id(0)
 
@@ -311,31 +318,40 @@
                     xbuf[128 * k : 128 * k + 128, (2 * i + j) * 128 : (2 * i + j + 1) * 128] = x[head, k, zz]
 
     def emit(ws):
-        w = jnp.concatenate([r[j] for r in ws for j in range(2)], axis=0)
-        part = jnp.dot(xbuf[...], w, preferred_element_type=jnp.float32).astype(jnp.bfloat16)
+        acc = None
         for i in range(4):
-            out[i] = part[:, 128 * i : 128 * (i + 1)]
-
-    @pl.when(step // 4 == c)
+            w = ws[i][...].reshape(256, OUT_COLS) if i < 3 else jnp.concatenate([ws[3][0], ws[4][0]], axis=0)
+            part = jnp.dot(xbuf[:, 256 * i : 256 * (i + 1)], w, preferred_element_type=jnp.float32)
+            acc = part if acc is None else acc + part
+        acc = acc.astype(jnp.bfloat16)
+        for i in range(OUT_COLS // 128):
+            out[i] = acc[:, 128 * i : 128 * (i + 1)]
+
+    @pl.when(step // OUT_STEPS == c)
     def _():
         emit(mine)
 
-    @pl.when(step // 4 != c)
+    @pl.when(step // OUT_STEPS != c)
     def _():
         emit(other)
 
 
 def out_project(idx, x, mine, other):
-    def columns(which):
-        return pl.BlockSpec((2, 128, 512), lambda i, s: (0, 0, jnp.clip(i - 4 * which(s[4]), 0, 3)))
+    def columns(w, which):
+        return pl.BlockSpec(
+            (w.shape[0], 128, OUT_COLS),
+            lambda i, s: (0, 0, jnp.clip(i - OUT_STEPS * which(s[4]), 0, OUT_STEPS - 1)),
+        )
 
     return pl.pallas_call(
         out_kernel,
         grid_spec=pltpu.PrefetchScalarGridSpec(
             num_scalar_prefetch=1,
-            grid=(8,),
-            in_specs=[whole(x)] + [columns(lambda c: c)] * 4 + [columns(lambda c: 1 - c)] * 4,
-            out_specs=pl.BlockSpec((4, 256, 128), lambda i, s: (i, 0, 0)),
+            grid=(2 * OUT_STEPS,),
+            in_specs=[whole(x)]
+            + [columns(w, lambda c: c) for w in mine]
+            + [columns(w, lambda c: 1 - c) for w in other],
+            out_specs=pl.BlockSpec((OUT_COLS // 128, 256, 128), lambda i, s: (i, 0, 0)),
             scratch_shapes=[pltpu.VMEM((256, 1024), jnp.bfloat16)],
         ),
         out_shape=jax.ShapeDtypeStruct((32, 256, 128), jnp.bfloat16),
@@ -377,7 +393,15 @@
 
     positions = ((xl * 2 + c) * tok + jnp.arange(tok, dtype=jnp.int32)).astype(jnp.float32)
     cosine, sine = rope_tables(positions, head)
+
+    w_half = lax.dynamic_slice_in_dim(w_out, c * half, half, 1)
+    w_pair = jnp.stack([w_half, lax.ppermute(w_half, ("xl", "xh"), CROSS)])
+
     acc, w_near_far = project_near(idx, near_a + near_b, w_loc, w_own, w_oth)
+
+    w_pair, acc = lax.optimization_barrier((w_pair, acc))
+    w_before = permute(w_pair, "z", 1)
+    w_after = permute(w_pair, "z", -1)
 
     keep_a, keep_b, send, ssq = project_far(
         idx, (*far_a, *far_b), acc, w_near_far, gains, cosine, sine
@@ -389,36 +413,31 @@
     ssq = to_all(ssq[None], ("z", "y")).sum(axis=0)
     inverse = lax.rsqrt(ssq / width + EPS)
 
-    w_half = lax.dynamic_slice_in_dim(w_out, c * half, half, 1)
-    w_pair = jnp.stack([w_half, lax.ppermute(w_half, ("xl", "xh"), CROSS)])
-    w_pair, inverse = lax.optimization_barrier((w_pair, inverse))
-    w_before = permute(w_pair, "z", 1)
-    w_after = permute(w_pair, "z", -1)
-    w_far = permute(w_pair, "z", 2)
-
-    near = jnp.stack([inverse, swap(inverse, "xl")])
-    other = swap(near, "c")
-    partner = swap(inverse, "xh")
-    low, high = jnp.where(xh == 0, inverse, partner), jnp.where(xh == 0, partner, inverse)
-    qk_scale = jnp.stack([low, high], axis=1)
+    scales = (inverse, exchange(inverse, ("xl",)), exchange(inverse, ("c",)), exchange(inverse, ("xl", "c")))
+    w_before, w_after, inverse = lax.optimization_barrier((w_before, w_after, inverse))
+    w_far_low = permute(w_before[:1], "z", 1)
+    w_far_high = permute(w_after[1:], "z", -1)
 
     d_recv = swap(recv[tok // 2 :], "c")
 
-    attended, top = attend(idx, keep_a, keep_b, recv, d_own, d_recv, near, other)
-
-    attended, w_before, w_after, w_far = lax.optimization_barrier((attended, w_before, w_after, w_far))
-    w_mine = (w_pair, w_before, w_after, w_far)
+    attended, top = attend(idx, keep_a, keep_b, recv, d_own, d_recv, *scales)
+
+    w_mine = (w_pair, w_before, w_after, w_far_low, w_far_high)
     w_other = tuple(swap(w, "c") for w in w_mine)
 
     attended = attended.reshape(16, 128, 128)
     attended = lax.all_to_all(attended, ("xl", "c", "z"), 0, 0, tiled=True)
     partial_out = out_project(idx, attended.reshape(2, 2, 4, 128, 128), w_mine, w_other)
+    partial_out, top, inverse = lax.optimization_barrier((partial_out, top, inverse))
     pieces = lax.all_to_all(partial_out, TENSOR, 0, 0, tiled=True)
     pieces = pieces.reshape(4, 4, 2, 2, 128, 128).astype(jnp.float32).sum(axis=1)
     pieces = jnp.where(c == 0, pieces, pieces[:, :, ::-1])
     mixed = pieces.transpose(1, 2, 0, 3, 4).reshape(seqs, tok, head).astype(jnp.bfloat16)
     tops = to_all(top[:1] * (1.0 / LOG2E), ("xl", "c", "xh")).reshape(2, 2, 2, 128)
     peak = lax.dynamic_index_in_dim(tops, xh, 0, keepdims=False).max(axis=(0, 1))[:1]
+    partner = swap(inverse, "xh")
+    low, high = jnp.where(xh == 0, inverse, partner), jnp.where(xh == 0, partner, inverse)
+    qk_scale = jnp.stack([low, high], axis=1)
     return (mixed, peak, qk_scale)
 
 

time: 231 us -> 240 us (1.039)
  blocking collectives: 0 us -> 26.3 us
  waiting for transfers between devices: 94.5 us -> 83 us
  starting transfers between devices: 72.5 us -> 68.2 us
    all_to_all x0 -> x2, blocking collectives: none -> 26.3 us  [to_all(): lax.all_to_all(jnp.broadcast_to(array, (size, *array.shape[1:])), axes, 0...]
    all_to_all x2 -> x0, starting transfers between devices: 9.56 us -> none  [to_all(): lax.all_to_all(jnp.broadcast_to(array, (size, *array.shape[1:])), axes, 0...]
    ppermute x21 -> x22, waiting for transfers between devices: 42.9 us -> 34.6 us  [permute(): return lax.ppermute(array, axis, shift(4, k))]
    all_to_all x2 -> x0, waiting for transfers between devices: 5.24 us -> none  [to_all(): lax.all_to_all(jnp.broadcast_to(array, (size, *array.shape[1:])), axes, 0...]
    ppermute x0 -> x3, starting transfers between devices: none -> 2.93 us  [exchange(): return lax.ppermute(array, axes, [(i, n - 1 - i) for i in range(n)])]
    ppermute x21 -> x22, starting transfers between devices: 29.2 us -> 31.7 us  [permute(): return lax.ppermute(array, axis, shift(4, k))]
    ppermute x13 -> x12, waiting for transfers between devices: 33.4 us -> 34.2 us  [swap(): return lax.ppermute(array, axis, [(0, 1), (1, 0)])]
    ppermute x13 -> x12, starting transfers between devices: 20.3 us -> 20 us  [swap(): return lax.ppermute(array, axis, [(0, 1), (1, 0)])]
  transfers between devices with their start and end apart: 40 -> 41, of which waited for: 17 -> 16; matrix products, arithmetic and copies ran while one was open for 6% -> 5% of each run, Pallas kernels for 18% -> 11%
where the time goes in v2:
time: 240 us; the launch traced here: 239 us
  waiting for transfers between devices  83 us (35%)
  starting transfers between devices  68.2 us (28%)
  Pallas kernels  39.9 us (17%)
  blocking collectives  26.3 us (11%)
  local copies, waits for them, and re-layouts  11.5 us (5%)
  other arithmetic  8.86 us (4%)
    ppermute x22, waiting for transfers between devices, permute(): return lax.ppermute(array, axis, shift(4, k))  34.6 us
    ppermute x12, waiting for transfers between devices, swap(): return lax.ppermute(array, axis, [(0, 1), (1, 0)])  34.2 us
    ppermute x22, starting transfers between devices, permute(): return lax.ppermute(array, axis, shift(4, k))  31.7 us
    all_to_all x2, blocking collectives, to_all(): lax.all_to_all(jnp.broadcast_to(array, (size, *array.shape[1:])), axes, 0...  26.3 us
    ppermute x12, starting transfers between devices, swap(): return lax.ppermute(array, axis, [(0, 1), (1, 0)])  20 us
    pallas_call x1, Pallas kernels, attend(): pl.pallas_call(attend_kernel, grid_spec=pltpu.PrefetchScalarGridSpec(num_...  15 us
    pallas_call x1, Pallas kernels, project_near(): pl.pallas_call(near_kernel, grid_spec=pltpu.PrefetchScalarGridSpec(num_sc...  12.2 us
    all_to_all x1, waiting for transfers between devices, layer(): attended = lax.all_to_all(attended, ('xl', 'c', 'z'), 0, 0, tiled=True)  10.2 us
  transfers between devices with their start and end apart: 41, of which 16 were waited for; matrix products, arithmetic and copies ran while one was open for 5% of the time, Pallas kernels for 11%

profile of v2, /device:TPU:1, one launch (start us, length us, event | category | flops | bytes accessed | tf_op | source)
XLA Modules:
  0.0 238.8 jit_solution(6340937648542168386)
XLA Ops:
  3.4 3.3 %collective-permute-start.20 = (bf16[3,2048,128]{2,1,0:T(8,128)(2,1)}, bf16[3,2048,128]{2,1,0:T(8,128)(2,1)}, u32[]{:S(2)}, u32[]{:S(2)}) collective-permute-start(bf16[3,2048,128]{2,1,0:T(8,128)(2,1)} %dynamic-slice_bitcast_fusion), channel_id=1, source_target_pairs={{0,65},{65,0},{1,64},{64,1},{2,67},{67,2},{3,66},{66,3},{4,69},{69... | collective-permute-start | bytes 4718600 | tf_op jit(solution)/shard_map/ppermute | solution.py:384
  7.4 3.8 %collective-permute-start.3 = (bf16[1024,128]{1,0:T(8,128)(2,1)S(1)}, bf16[1024,128]{1,0:T(8,128)(2,1)S(1)}, u32[]{:S(2)}, u32[]{:S(2)}) collective-permute-start(bf16[1024,128]{1,0:T(8,128)(2,1)S(1)} %bitcast.42), channel_id=1, source_target_pairs={{0,24},{8,0},{16,8},{24,16},{1,25},{9,1},{17,9},{25,17},{2,26},{10... | collective-permute-start | bytes 786440 | tf_op jit(solution)/shard_map/ppermute | solution.py:44
  11.8 3.5 %collective-permute-done.7 = bf16[1024,128]{1,0:T(8,128)(2,1)S(1)} collective-permute-done((bf16[1024,128]{1,0:T(8,128)(2,1)S(1)}, bf16[1024,128]{1,0:T(8,128)(2,1)S(1)}, u32[]{:S(2)}, u32[]{:S(2)}) %collective-permute-start.7) | collective-permute-done | bytes 262176 | tf_op jit(solution)/shard_map/ppermute | solution.py:30
  29.0 3.2 %collective-permute-start.13 = (bf16[2,1024,128]{2,1,0:T(8,128)(2,1)S(1)}, bf16[2,1024,128]{2,1,0:T(8,128)(2,1)}, u32[]{:S(2)}, u32[]{:S(2)}) collective-permute-start(bf16[2,1024,128]{2,1,0:T(8,128)(2,1)S(1)} %pad_maximum_fusion.4.refs_7_), channel_id=1, source_target_pairs={{0,24},{8,0},{16,8},{24,16},{1,25},{9,1},{17,9},{25,17},{2,26},{10... | collective-permute-start | bytes 1572872 | tf_op jit(solution)/shard_map/ppermute | solution.py:44
  35.5 6.1 %collective-permute-done.5.refs_5_ = bf16[2,1024,128]{2,1,0:T(8,128)(2,1)} collective-permute-done((bf16[2,1024,128]{2,1,0:T(8,128)(2,1)S(1)}, bf16[2,1024,128]{2,1,0:T(8,128)(2,1)}, u32[]{:S(2)}, u32[]{:S(2)}) %collective-permute-start.5) | collective-permute-done | bytes 524320 | tf_op jit(solution)/shard_map/ppermute | solution.py:44
  48.6 3.6 %collective-permute-start.21 = (bf16[3,2048,128]{2,1,0:T(8,128)(2,1)}, bf16[3,2048,128]{2,1,0:T(8,128)(2,1)}, u32[]{:S(2)}, u32[]{:S(2)}) collective-permute-start(bf16[3,2048,128]{2,1,0:T(8,128)(2,1)} %collective-permute-done.20.refs_13_), channel_id=1, source_target_pairs={{0,32},{32,0},{1,33},{33,1},{2,34},{34,2},{3,35},{35,3},{4,36},{36... | collective-permute-start | bytes 4718600 | tf_op jit(solution)/shard_map/ppermute | solution.py:30
  58.5 4.0 %collective-permute-start.19 = (bf16[2,1024,128]{2,1,0:T(8,128)(2,1)S(1)}, bf16[2,1024,128]{2,1,0:T(8,128)(2,1)}, u32[]{:S(2)}, u32[]{:S(2)}) collective-permute-start(bf16[2,1024,128]{2,1,0:T(8,128)(2,1)S(1)} %pad_maximum_fusion.3.refs_6_), channel_id=1, source_target_pairs={{0,24},{8,0},{16,8},{24,16},{1,25},{9,1},{17,9},{25,17},{2,26},{10... | collective-permute-start | bytes 1572872 | tf_op jit(solution)/shard_map/ppermute | solution.py:44
  62.5 3.2 %fusion.2 = (f32[1024,64]{1,0:T(8,128)}, f32[1024,64]{1,0:T(8,128)}, f32[1024,64]{1,0:T(8,128)}) fusion(f32[64]{0:T(128)S(1)} %multiply_power_fusion, f32[1024]{0:T(1024)S(1)} %add_convert_fusion), kind=kLoop, calls=%fused_computation.15 | loop fusion | flops 131072 | bytes 790784 | tf_op jit(solution)/shard_map/neg | solution.py:370
  65.7 3.3 %collective-permute-done.16.refs_3_ = bf16[2,1024,128]{2,1,0:T(8,128)(2,1)} collective-permute-done((bf16[2,1024,128]{2,1,0:T(8,128)(2,1)S(1)}, bf16[2,1024,128]{2,1,0:T(8,128)(2,1)}, u32[]{:S(2)}, u32[]{:S(2)}) %collective-permute-start.16) | collective-permute-done | bytes 524320 | tf_op jit(solution)/shard_map/ppermute | solution.py:44
  76.9 12.2 %project_near.1 = (f32[1024,768]{1,0:T(8,128)S(1)}, bf16[1024,768]{1,0:T(8,128)(2,1)S(1)}) custom-call(s32[5]{0:T(128)S(1)} %stack.84.idx, bf16[2,1024,128]{2,1,0:T(8,128)(2,1)S(1)} %pad_maximum_fusion.1.refs_0_, bf16[2,1024,128]{2,1,0:T(8,128)(2,1)S(1)} %pad_maximum_fusion.2.refs_1_, bf16[2,1024,128]{2,1,0:T(8,128)(2,1)} %collective-permute-done.1.refs_2_, ...), custom_call_target="tpu_custom_call" | custom-call | tf_op jit(solution)/shard_map/project_near/pallas_call | solution.py:173
  89.2 5.2 %project_far.1 = (bf16[512,128]{1,0:T(8,128)(2,1)S(1)}, bf16[2560,128]{1,0:T(8,128)(2,1)S(1)}, bf16[3072,128]{1,0:T(8,128)(2,1)S(1)}, f32[2,1024]{1,0:T(2,128)S(1)}) custom-call(s32[5]{0:T(128)S(1)} %stack.84.idx, bf16[2,1024,128]{2,1,0:T(8,128)(2,1)} %collective-permute-done.2.refs_0_, bf16[2,1024,128]{2,1,0:T(8,128)(2,1)} %collective-permute-done.6.refs_1_, ...), custom_call_target="tpu_custom_call" | custom-call | tf_op jit(solution)/shard_map/project_far/pallas_call | solution.py:205
  98.1 4.2 %collective-permute-start.24 = (bf16[2560,128]{1,0:T(8,128)(2,1)S(1)}, bf16[2560,128]{1,0:T(8,128)(2,1)}, u32[]{:S(2)}, u32[]{:S(2)}) collective-permute-start(bf16[2560,128]{1,0:T(8,128)(2,1)S(1)} %get-tuple-element.25.keep_b), channel_id=1, source_target_pairs={{0,32},{32,0},{1,33},{33,1},{2,34},{34,2},{3,35},{35,3},{4,36},{36... | collective-permute-start | bytes 1966088 | tf_op jit(solution)/shard_map/ppermute | solution.py:30
  102.2 8.3 %collective-permute-done.23.recv = bf16[3072,128]{1,0:T(8,128)(2,1)S(1)} collective-permute-done((bf16[3072,128]{1,0:T(8,128)(2,1)S(1)}, bf16[3072,128]{1,0:T(8,128)(2,1)S(1)}, u32[]{:S(2)}, u32[]{:S(2)}) %collective-permute-start.23) | collective-permute-done | bytes 786464 | tf_op jit(solution)/shard_map/ppermute | solution.py:30
  111.4 4.5 %collective-permute-start.25 = (bf16[2560,128]{1,0:T(8,128)(2,1)}, bf16[2560,128]{1,0:T(8,128)(2,1)}, u32[]{:S(2)}, u32[]{:S(2)}) collective-permute-start(bf16[2560,128]{1,0:T(8,128)(2,1)} %slice.20), channel_id=1, source_target_pairs={{0,32},{32,0},{1,33},{33,1},{2,34},{34,2},{3,35},{35,3},{4,36},{36... | collective-permute-start | bytes 1966088 | tf_op jit(solution)/shard_map/ppermute | solution.py:30
  116.0 15.0 %all_to_all.21 = f32[16,2,1024]{2,1,0:T(2,128)} all-to-all(f32[16,2,1024]{2,1,0:T(2,128)S(1)} %broadcast_in_dim.4), channel_id=1, replica_groups=mesh['xl'=2,'c'=2,'z'=4,'y'=4,'xh'=2] {'z','y'}, dimensions={0} | all-to-all | bytes 262144 | tf_op jit(solution)/shard_map/all_to_all | solution.py:35
  142.4 11.3 %collective-permute-done.31.refs_3_ = bf16[1,128,2048]{2,1,0:T(8,128)(2,1)} collective-permute-done((bf16[1,128,2048]{2,1,0:T(8,128)(2,1)S(1)}, bf16[1,128,2048]{2,1,0:T(8,128)(2,1)}, u32[]{:S(2)}, u32[]{:S(2)}) %collective-permute-start.31) | collective-permute-done | bytes 524320 | tf_op jit(solution)/shard_map/ppermute | solution.py:44
  154.6 15.0 %attend.1 = (bf16[4,512,128]{2,1,0:T(8,128)(2,1)S(1)}, f32[8,128]{1,0:T(8,128)S(1)}) custom-call(s32[5]{0:T(128)S(1)} %stack.84.idx, bf16[512,128]{1,0:T(8,128)(2,1)S(1)} %copy-done.7, bf16[2560,128]{1,0:T(8,128)(2,1)S(1)} %get-tuple-element.25.keep_b, bf16[3072,128]{1,0:T(8,128)(2,1)S(1)} %collective-permute-done.23.recv, ...), custom_call_target="tpu_custom_call" | custom-call | tf_op jit(solution)/shard_map/attend/pallas_call | solution.py:279
  170.4 4.4 %all-to-all-start.1 = ((bf16[16,128,128]{2,1,0:T(8,128)(2,1)}), bf16[16,128,128]{2,1,0:T(8,128)(2,1)S(1)}, u32[]{:S(2)}, u32[]{:S(2)}) async-start(bf16[16,128,128]{2,1,0:T(8,128)(2,1)} %bitcast.39), calls=%async_computation.1 | async-start | bytes 1048576 | tf_op jit(solution)/shard_map/all_to_all | solution.py:429
  174.8 10.2 %all-to-all-done.1 = bf16[16,128,128]{2,1,0:T(8,128)(2,1)S(1)} async-done(((bf16[16,128,128]{2,1,0:T(8,128)(2,1)}), bf16[16,128,128]{2,1,0:T(8,128)(2,1)S(1)}, u32[]{:S(2)}, u32[]{:S(2)}) %all-to-all-start.1) | async-done | bytes 524320 | tf_op jit(solution)/shard_map/all_to_all | solution.py:429
  185.0 7.5 %out_project.1 = bf16[32,256,128]{2,1,0:T(8,128)(2,1)} custom-call(s32[5]{0:T(128)S(1)} %stack.84.idx, bf16[2,2,4,128,128]{4,3,2,1,0:T(8,128)(2,1)S(1)} %bitcast.38, bf16[2,128,2048]{2,1,0:T(8,128)(2,1)S(1)} %pad_maximum_fusion.refs_0_, bf16[2,128,2048]{2,1,0:T(8,128)(2,1)} %collective-permute-done.29.refs_1_, ...), custom_call_target="tpu_custom_call" | custom-call | tf_op jit(solution)/shard_map/out_project/pallas_call | solution.py:346
  192.5 11.3 %all_to_all.22 = f32[8,1,128]{2,1,0:T(1,128)S(1)} all-to-all(f32[8,1,128]{2,1,0:T(1,128)S(1)} %broadcast_in_dim.5), channel_id=1, replica_groups=mesh['xl'=2,'c'=2,'z'=4,'y'=4,'xh'=2] {'xl','c','xh'}, dimensions={0} | all-to-all | bytes 8192 | tf_op jit(solution)/shard_map/all_to_all | solution.py:35
  203.7 4.0 %all-to-all-start.2 = ((bf16[32,256,128]{2,1,0:T(8,128)(2,1)}), bf16[32,256,128]{2,1,0:T(8,128)(2,1)S(1)}, u32[]{:S(2)}, u32[]{:S(2)}) async-start(bf16[32,256,128]{2,1,0:T(8,128)(2,1)} %out_project.1), calls=%async_computation.2 | async-start | bytes 4194304 | tf_op jit(solution)/shard_map/all_to_all | solution.py:432
  211.0 22.4 %collective-permute-done.38 = f32[2,1024]{1,0:T(2,128)S(1)} collective-permute-done((f32[2,1024]{1,0:T(2,128)S(1)}, f32[2,1024]{1,0:T(2,128)S(1)}, u32[]{:S(2)}, u32[]{:S(2)}) %collective-permute-start.38) | collective-permute-done | bytes 8224 | tf_op jit(solution)/shard_map/ppermute | solution.py:30
  234.0 3.4 %all-to-all-done.2 = bf16[32,256,128]{2,1,0:T(8,128)(2,1)S(1)} async-done(((bf16[32,256,128]{2,1,0:T(8,128)(2,1)}), bf16[32,256,128]{2,1,0:T(8,128)(2,1)S(1)}, u32[]{:S(2)}, u32[]{:S(2)}) %all-to-all-start.2) | async-done | bytes 2097184 | tf_op jit(solution)/shard_map/all_to_all | solution.py:432
  (123 shorter events, 65.0 us)
Async XLA Ops:
  3.4 45.2 %collective-permute-start.20 = (bf16[3,2048,128]{2,1,0:T(8,128)(2,1)}, bf16[3,2048,128]{2,1,0:T(8,128)(2,1)}, u32[]{:S(2)}, u32[]{:S(2)}) collective-permute-start(bf16[3,2048,128]{2,1,0:T(8,128)(2,1)} %dynamic-slice_bitcast_fusion), channel_id=1, source_target_pairs={{0,65},{65,0},{1,64},{64,1},{2,67},{67,2},{3,66},{66,3},{4,69},{69... | collective-permute-start | bytes 4718600 | tf_op jit(solution)/shard_map/ppermute | solution.py:384
  11.1 14.9 %collective-permute-start = (bf16[1024,128]{1,0:T(8,128)(2,1)S(1)}, bf16[1024,128]{1,0:T(8,128)(2,1)S(1)}, u32[]{:S(2)}, u32[]{:S(2)}) collective-permute-start(bf16[1024,128]{1,0:T(8,128)(2,1)S(1)} %bitcast.44), channel_id=1, source_target_pairs={{0,8},{8,16},{16,24},{24,0},{1,9},{9,17},{17,25},{25,1},{2,10},{10... | collective-permute-start | bytes 786440 | tf_op jit(solution)/shard_map/ppermute | solution.py:44
  26.0 15.5 %collective-permute-start.5 = (bf16[2,1024,128]{2,1,0:T(8,128)(2,1)S(1)}, bf16[2,1024,128]{2,1,0:T(8,128)(2,1)}, u32[]{:S(2)}, u32[]{:S(2)}) collective-permute-start(bf16[2,1024,128]{2,1,0:T(8,128)(2,1)S(1)} %pad_maximum_fusion.2.refs_1_), channel_id=1, source_target_pairs={{0,6},{2,0},{4,2},{6,4},{1,7},{3,1},{5,3},{7,5},{8,14},{10,8},{12,... | collective-permute-start | bytes 1572872 | tf_op jit(solution)/shard_map/ppermute | solution.py:44
  28.8 17.7 %collective-permute-start.1 = (bf16[2,1024,128]{2,1,0:T(8,128)(2,1)S(1)}, bf16[2,1024,128]{2,1,0:T(8,128)(2,1)}, u32[]{:S(2)}, u32[]{:S(2)}) collective-permute-start(bf16[2,1024,128]{2,1,0:T(8,128)(2,1)S(1)} %pad_maximum_fusion.1.refs_0_), channel_id=1, source_target_pairs={{0,2},{2,4},{4,6},{6,0},{1,3},{3,5},{5,7},{7,1},{8,10},{10,12},{12... | collective-permute-start | bytes 1572872 | tf_op jit(solution)/shard_map/ppermute | solution.py:44
  29.0 17.5 %collective-permute-start.13 = (bf16[2,1024,128]{2,1,0:T(8,128)(2,1)S(1)}, bf16[2,1024,128]{2,1,0:T(8,128)(2,1)}, u32[]{:S(2)}, u32[]{:S(2)}) collective-permute-start(bf16[2,1024,128]{2,1,0:T(8,128)(2,1)S(1)} %pad_maximum_fusion.4.refs_7_), channel_id=1, source_target_pairs={{0,24},{8,0},{16,8},{24,16},{1,25},{9,1},{17,9},{25,17},{2,26},{10... | collective-permute-start | bytes 1572872 | tf_op jit(solution)/shard_map/ppermute | solution.py:44
  41.6 16.2 %collective-permute-start.15 = (bf16[128,2048]{1,0:T(8,128)(2,1)S(1)}, bf16[128,2048]{1,0:T(8,128)(2,1)S(1)}, u32[]{:S(2)}, u32[]{:S(2)}) collective-permute-start(bf16[128,2048]{1,0:T(8,128)(2,1)S(1)} %constant_dynamic-slice_fusion), channel_id=1, source_target_pairs={{0,65},{65,0},{1,64},{64,1},{2,67},{67,2},{3,66},{66,3},{4,69},{69... | collective-permute-start | bytes 1572872 | tf_op jit(solution)/shard_map/ppermute | solution.py:398
  48.6 27.4 %collective-permute-start.21 = (bf16[3,2048,128]{2,1,0:T(8,128)(2,1)}, bf16[3,2048,128]{2,1,0:T(8,128)(2,1)}, u32[]{:S(2)}, u32[]{:S(2)}) collective-permute-start(bf16[3,2048,128]{2,1,0:T(8,128)(2,1)} %collective-permute-done.20.refs_13_), channel_id=1, source_target_pairs={{0,32},{32,0},{1,33},{33,1},{2,34},{34,2},{3,35},{35,3},{4,36},{36... | collective-permute-start | bytes 4718600 | tf_op jit(solution)/shard_map/ppermute | solution.py:30
  69.0 20.2 %collective-permute-start.6 = (bf16[2,1024,128]{2,1,0:T(8,128)(2,1)}, bf16[2,1024,128]{2,1,0:T(8,128)(2,1)}, u32[]{:S(2)}, u32[]{:S(2)}) collective-permute-start(bf16[2,1024,128]{2,1,0:T(8,128)(2,1)} %collective-permute-done.5.refs_5_), channel_id=1, source_target_pairs={{0,6},{2,0},{4,2},{6,4},{1,7},{3,1},{5,3},{7,5},{8,14},{10,8},{12,... | collective-permute-start | bytes 1572872 | tf_op jit(solution)/shard_map/ppermute | solution.py:44
  69.5 19.7 %collective-permute-start.2 = (bf16[2,1024,128]{2,1,0:T(8,128)(2,1)}, bf16[2,1024,128]{2,1,0:T(8,128)(2,1)}, u32[]{:S(2)}, u32[]{:S(2)}) collective-permute-start(bf16[2,1024,128]{2,1,0:T(8,128)(2,1)} %collective-permute-done.1.refs_2_), channel_id=1, source_target_pairs={{0,2},{2,4},{4,6},{6,0},{1,3},{3,5},{5,7},{7,1},{8,10},{10,12},{12... | collective-permute-start | bytes 1572872 | tf_op jit(solution)/shard_map/ppermute | solution.py:44
  71.1 18.1 %collective-permute-start.14 = (bf16[2,1024,128]{2,1,0:T(8,128)(2,1)}, bf16[2,1024,128]{2,1,0:T(8,128)(2,1)}, u32[]{:S(2)}, u32[]{:S(2)}) collective-permute-start(bf16[2,1024,128]{2,1,0:T(8,128)(2,1)} %collective-permute-done.13.refs_11_), channel_id=1, source_target_pairs={{0,24},{8,0},{16,8},{24,16},{1,25},{9,1},{17,9},{25,17},{2,26},{10... | collective-permute-start | bytes 1572872 | tf_op jit(solution)/shard_map/ppermute | solution.py:44
  72.3 16.8 %collective-permute-start.10 = (bf16[2,1024,128]{2,1,0:T(8,128)(2,1)}, bf16[2,1024,128]{2,1,0:T(8,128)(2,1)}, u32[]{:S(2)}, u32[]{:S(2)}) collective-permute-start(bf16[2,1024,128]{2,1,0:T(8,128)(2,1)} %collective-permute-done.9.refs_8_), channel_id=1, source_target_pairs={{0,8},{8,16},{16,24},{24,0},{1,9},{9,17},{17,25},{25,1},{2,10},{10... | collective-permute-start | bytes 1572872 | tf_op jit(solution)/shard_map/ppermute | solution.py:44
  95.1 15.4 %collective-permute-start.23 = (bf16[3072,128]{1,0:T(8,128)(2,1)S(1)}, bf16[3072,128]{1,0:T(8,128)(2,1)S(1)}, u32[]{:S(2)}, u32[]{:S(2)}) collective-permute-start(bf16[3072,128]{1,0:T(8,128)(2,1)S(1)} %get-tuple-element.26), channel_id=1, source_target_pairs={{0,64},{64,0},{1,65},{65,1},{2,66},{66,2},{3,67},{67,3},{4,68},{68... | collective-permute-start | bytes 2359304 | tf_op jit(solution)/shard_map/ppermute | solution.py:30
  95.1 38.5 %collective-permute-start.29 = (bf16[2,128,2048]{2,1,0:T(8,128)(2,1)S(1)}, bf16[2,128,2048]{2,1,0:T(8,128)(2,1)}, u32[]{:S(2)}, u32[]{:S(2)}) collective-permute-start(bf16[2,128,2048]{2,1,0:T(8,128)(2,1)S(1)} %pad_maximum_fusion.refs_0_), channel_id=1, source_target_pairs={{0,8},{8,16},{16,24},{24,0},{1,9},{9,17},{17,25},{25,1},{2,10},{10... | collective-permute-start | bytes 3145736 | tf_op jit(solution)/shard_map/ppermute | solution.py:44
  96.4 38.6 %collective-permute-start.30 = (bf16[2,128,2048]{2,1,0:T(8,128)(2,1)S(1)}, bf16[2,128,2048]{2,1,0:T(8,128)(2,1)}, u32[]{:S(2)}, u32[]{:S(2)}) collective-permute-start(bf16[2,128,2048]{2,1,0:T(8,128)(2,1)S(1)} %pad_maximum_fusion.refs_0_), channel_id=1, source_target_pairs={{0,24},{8,0},{16,8},{24,16},{1,25},{9,1},{17,9},{25,17},{2,26},{10... | collective-permute-start | bytes 3145736 | tf_op jit(solution)/shard_map/ppermute | solution.py:44
  98.1 43.5 %collective-permute-start.24 = (bf16[2560,128]{1,0:T(8,128)(2,1)S(1)}, bf16[2560,128]{1,0:T(8,128)(2,1)}, u32[]{:S(2)}, u32[]{:S(2)}) collective-permute-start(bf16[2560,128]{1,0:T(8,128)(2,1)S(1)} %get-tuple-element.25.keep_b), channel_id=1, source_target_pairs={{0,32},{32,0},{1,33},{33,1},{2,34},{34,2},{3,35},{35,3},{4,36},{36... | collective-permute-start | bytes 1966088 | tf_op jit(solution)/shard_map/ppermute | solution.py:30
  111.4 30.9 %collective-permute-start.25 = (bf16[2560,128]{1,0:T(8,128)(2,1)}, bf16[2560,128]{1,0:T(8,128)(2,1)}, u32[]{:S(2)}, u32[]{:S(2)}) collective-permute-start(bf16[2560,128]{1,0:T(8,128)(2,1)} %slice.20), channel_id=1, source_target_pairs={{0,32},{32,0},{1,33},{33,1},{2,34},{34,2},{3,35},{35,3},{4,36},{36... | collective-permute-start | bytes 1966088 | tf_op jit(solution)/shard_map/ppermute | solution.py:30
  138.4 36.4 %collective-permute-start.33 = (bf16[2,128,2048]{2,1,0:T(8,128)(2,1)S(1)}, bf16[2,128,2048]{2,1,0:T(8,128)(2,1)}, u32[]{:S(2)}, u32[]{:S(2)}) collective-permute-start(bf16[2,128,2048]{2,1,0:T(8,128)(2,1)S(1)} %pad_maximum_fusion.refs_0_), channel_id=1, source_target_pairs={{0,32},{32,0},{1,33},{33,1},{2,34},{34,2},{3,35},{35,3},{4,36},{36... | collective-permute-start | bytes 3145736 | tf_op jit(solution)/shard_map/ppermute | solution.py:30
  139.0 15.7 %collective-permute-start.32 = (bf16[1,128,2048]{2,1,0:T(8,128)(2,1)S(1)}, bf16[1,128,2048]{2,1,0:T(8,128)(2,1)}, u32[]{:S(2)}, u32[]{:S(2)}) collective-permute-start(bf16[1,128,2048]{2,1,0:T(8,128)(2,1)S(1)} %slice.17), channel_id=1, source_target_pairs={{0,24},{8,0},{16,8},{24,16},{1,25},{9,1},{17,9},{25,17},{2,26},{10... | collective-permute-start | bytes 1572872 | tf_op jit(solution)/shard_map/ppermute | solution.py:44
  141.6 43.3 %collective-permute-start.34 = (bf16[2,128,2048]{2,1,0:T(8,128)(2,1)}, bf16[2,128,2048]{2,1,0:T(8,128)(2,1)}, u32[]{:S(2)}, u32[]{:S(2)}) collective-permute-start(bf16[2,128,2048]{2,1,0:T(8,128)(2,1)} %collective-permute-done.29.refs_1_), channel_id=1, source_target_pairs={{0,32},{32,0},{1,33},{33,1},{2,34},{34,2},{3,35},{35,3},{4,36},{36... | collective-permute-start | bytes 3145736 | tf_op jit(solution)/shard_map/ppermute | solution.py:30
  142.3 42.7 %collective-permute-start.35 = (bf16[2,128,2048]{2,1,0:T(8,128)(2,1)}, bf16[2,128,2048]{2,1,0:T(8,128)(2,1)}, u32[]{:S(2)}, u32[]{:S(2)}) collective-permute-start(bf16[2,128,2048]{2,1,0:T(8,128)(2,1)} %collective-permute-done.30.refs_2_), channel_id=1, source_target_pairs={{0,32},{32,0},{1,33},{33,1},{2,34},{34,2},{3,35},{35,3},{4,36},{36... | collective-permute-start | bytes 3145736 | tf_op jit(solution)/shard_map/ppermute | solution.py:30
  153.7 31.3 %collective-permute-start.36 = (bf16[1,128,2048]{2,1,0:T(8,128)(2,1)}, bf16[1,128,2048]{2,1,0:T(8,128)(2,1)}, u32[]{:S(2)}, u32[]{:S(2)}) collective-permute-start(bf16[1,128,2048]{2,1,0:T(8,128)(2,1)} %collective-permute-done.31.refs_3_), channel_id=1, source_target_pairs={{0,32},{32,0},{1,33},{33,1},{2,34},{34,2},{3,35},{35,3},{4,36},{36... | collective-permute-start | bytes 1572872 | tf_op jit(solution)/shard_map/ppermute | solution.py:30
  154.6 30.4 %collective-permute-start.37 = (bf16[1,128,2048]{2,1,0:T(8,128)(2,1)}, bf16[1,128,2048]{2,1,0:T(8,128)(2,1)}, u32[]{:S(2)}, u32[]{:S(2)}) collective-permute-start(bf16[1,128,2048]{2,1,0:T(8,128)(2,1)} %collective-permute-done.32.refs_4_), channel_id=1, source_target_pairs={{0,32},{32,0},{1,33},{33,1},{2,34},{34,2},{3,35},{35,3},{4,36},{36... | collective-permute-start | bytes 1572872 | tf_op jit(solution)/shard_map/ppermute | solution.py:30
  203.7 33.7 %all-to-all-start.2 = ((bf16[32,256,128]{2,1,0:T(8,128)(2,1)}), bf16[32,256,128]{2,1,0:T(8,128)(2,1)S(1)}, u32[]{:S(2)}, u32[]{:S(2)}) async-start(bf16[32,256,128]{2,1,0:T(8,128)(2,1)} %out_project.1), calls=%async_computation.2 | async-start | bytes 4194304 | tf_op jit(solution)/shard_map/all_to_all | solution.py:432
  207.8 25.6 %collective-permute-start.38 = (f32[2,1024]{1,0:T(2,128)S(1)}, f32[2,1024]{1,0:T(2,128)S(1)}, u32[]{:S(2)}, u32[]{:S(2)}) collective-permute-start(f32[2,1024]{1,0:T(2,128)S(1)} %add_rsqrt_fusion.s0), channel_id=1, source_target_pairs={{0,1},{1,0},{2,3},{3,2},{4,5},{5,4},{6,7},{7,6},{8,9},{9,8},{10,11... | collective-permute-start | bytes 24584 | tf_op jit(solution)/shard_map/ppermute | solution.py:30
  (31 other events, 391.4 us)
